TPU v7x, 128 devices: a whole 4x4x4 slice. The times are simulated.
128 devices in a mesh: row: 8 (over x_hi, z), col: 8 (over y, x_lo), layer: 2 (over core).
Axes of the slice: x: 4 (x_hi: 2, x_lo: 2; x = x_hi * 2 + x_lo), y: 4, z: 4, core: 2. Of those that a mesh axis runs over, the one named last changes fastest.
Arguments:
- expression: bfloat16 [24576, 1024], P(('row', 'col'), 'layer'), may hold values from -240 to 240
Outputs:
- connectivity: float32 [24576], P(('row', 'col', 'layer'))
All inputs are finite; a program needn't handle non-finite values.
Results may differ from a plain program's by a relative error of at most 0.00048.
Values may be sent and summed in bfloat16 or wider, within the bound.
No kernel may reach another device: no remote copies, remote signals or barrier semaphores. Data moves between devices by JAX's collectives and lax.ppermute only.
A program may use at most 64 MiB of HBM per device.

v0:
```python
import functools
import itertools

import jax
import jax.numpy as jnp
from jax import lax
from jax.experimental import pallas as pl
from jax.experimental.pallas import tpu as pltpu
from jax.sharding import Mesh
from jax.sharding import PartitionSpec as P


S = 1024
N = 4
CHIP = ("x_hi", "z", "y", "x_lo")
ALL = CHIP + ("layer",)
epsilon = 1e-05
VMEM_BYTES = 16 * 2**20


OFFSETS = (
    ((0, 0, 0), None),
    ((1, 0, 1), None),
    ((3, 1, 0), None),
    ((0, 3, 3), None),
    ((0, 3, 0), None),
    ((0, 0, 1), None),
    ((0, 0, 3), None),
    ((2, 0, 1), (1, 0, 1)),
    ((2, 1, 0), (3, 1, 0)),
    ((0, 2, 3), (0, 3, 3)),
    ((3, 1, 3), (3, 1, 0)),
)
DELTA = tuple(d for d, _ in OFFSETS)
BLOCKS = len(DELTA)


def minus(a, b):
    return tuple((p - q) % N for p, q in zip(a, b))


def choose_pairs():
    pairs, done = [(0, 0, False)], {(0, 0, 0)}
    for j, i in itertools.product(range(BLOCKS), range(BLOCKS)):
        if i >= j:
            continue
        d = minus(DELTA[i], DELTA[j])
        if d not in done:
            e = minus((0, 0, 0), d)
            done |= {d, e}
            pairs.append((i, j, d != e))
    assert len(done) == N**3
    return tuple(pairs)


PAIRS = choose_pairs()


def place(x, y, z, c):
    return (((x // 2 * N + z) * N + y) * 2 + x % 2) * 2 + c


def chips():
    return itertools.product(range(N), range(N), range(N))


def fetch(value, d, flip=0):
    pairs = []
    for p in chips():
        q = tuple((a + b) % N for a, b in zip(p, d))
        for c in range(2):
            pairs.append((place(*q, c ^ flip), place(*p, c)))
    return lax.ppermute(value, ALL, pairs)


def deliver(value, d0, d1):
    pairs = []
    for p in chips():
        for c, d in enumerate((d0, d1)):
            q = tuple((a + b) % N for a, b in zip(p, d))
            pairs.append((place(*p, c), place(*q, c)))
    return lax.ppermute(value, ALL, pairs)


def stage_sums(old, new, pairs, last, *refs):
    refs = list(refs)
    raw = [(refs.pop(0), refs.pop(0)) for _ in new]
    where = {b: refs.pop(0) for b in old}
    before = refs.pop(0) if old else None
    if last:
        own_ref, keep_ref, give_ref = refs.pop(0), refs.pop(0), refs.pop(0)
    else:
        out_ref = refs.pop(0)
    where |= {b: refs.pop(0) for b in new}
    row_ref, col_ref = refs
    core = lax.axis_index("layer")
    genes = raw[0][0].shape[0]
    half = genes // 2
    mine = pl.ds(pl.multiple_of(core * half, half), half)
    for b, (lo_ref, hi_ref) in zip(new, raw):
        lo = lo_ref[...].astype(jnp.float32)
        hi = hi_ref[...].astype(jnp.float32)
        total = jnp.sum(lo, axis=1, keepdims=True) + jnp.sum(hi, axis=1, keepdims=True)
        squares = jnp.sum(lo * lo, axis=1, keepdims=True) + jnp.sum(
            hi * hi, axis=1, keepdims=True
        )
        average = total / S
        variance = squares / S - average * average
        scale = lax.rsqrt(variance + epsilon)
        where[b][:, : S // 2] = (((lo - average) * scale) * 0.03125).astype(jnp.bfloat16)
        where[b][:, S // 2 :] = (((hi - average) * scale) * 0.03125).astype(jnp.bfloat16)
    rows_of = sorted({j for _, j, both in pairs if both})
    cols_of = sorted({i for i, _, _ in pairs})
    begun = set()
    for i, j, both in pairs:
        t = lax.dot_general(
            where[j][...],
            where[i][mine, :],
            (((1,), (1,)), ((), ())),
            preferred_element_type=jnp.float32,
        )
        t = 1.0 + t
        t = t * t
        t = t * t
        t = t * t * t
        cols = jnp.sum(t.reshape(genes // 8, 8, half), axis=0)
        c = cols_of.index(i)
        if ("c", i) in begun:
            col_ref[c] += cols
        else:
            col_ref[c] = cols
            begun.add(("c", i))
        if both:
            r = rows_of.index(j)
            wide = jnp.concatenate(
                [t[:, 128:], jnp.zeros((genes, 256 - half), jnp.float32)], axis=1
            )
            part = t[:, :128] + wide
            if ("r", j) in begun:
                row_ref[r] += part
            else:
                row_ref[r] = part
                begun.add(("r", j))
    ones = jnp.ones((8, 128), jnp.float32)
    for b in range(BLOCKS):
        parts = [jnp.zeros((1, half), jnp.float32)] * 2
        if before is not None:
            parts = [before[h, pl.ds(b, 1), :] for h in range(2)]
        if b in rows_of:
            rows = lax.dot_general(
                ones,
                row_ref[rows_of.index(b)],
                (((1,), (1,)), ((), ())),
                precision=lax.Precision.HIGHEST,
                preferred_element_type=jnp.float32,
            )
            parts = [p + rows[:1, h * half : (h + 1) * half] for h, p in enumerate(parts)]
        if b in cols_of:
            cols = jnp.sum(col_ref[cols_of.index(b)], axis=0, keepdims=True)
            parts = [p + jnp.where(core == h, cols, 0.0) for h, p in enumerate(parts)]
        for h in range(2):
            if not last:
                out_ref[h, pl.ds(b, 1), :] = parts[h]
            elif b == 0:
                own_ref[pl.ds(h, 1), :] = parts[h] * (0.5**12)
            else:
                kept = jnp.where(core == (b - 1) // 5, 1.0, 0.0) * (0.5**12)
                row = pl.ds((b - 1) % 5, 1)
                if b <= 5:
                    keep_ref[h, row, :] = parts[h] * kept
                    give_ref[h, row, :] = parts[h] * (0.5**12 - kept)
                else:
                    keep_ref[h, row, :] += parts[h] * kept
                    give_ref[h, row, :] += parts[h] * (0.5**12 - kept)


def joined_sums(keep_ref, got_ref, *out_refs):
    for m, out_ref in enumerate(out_refs):
        for h in range(2):
            row = pl.ds(m, 1)
            out_ref[pl.ds(h, 1), :] = keep_ref[h, row, :] + got_ref[h, row, :]


def owner_sums(own_ref, *refs):
    *arrived, mine_ref, other_ref = refs
    total = own_ref[...]
    for ref in arrived:
        total += ref[...]
    first = lax.axis_index("layer") == 0
    mine_ref[...] = jnp.where(first, total[:1], total[1:])
    other_ref[...] = jnp.where(first, total[1:], total[:1])


STAGES = ((0, 1, 2, 3), (4, 5, 6), (7, 8, 9, 10))


def all_sums(raw, genes):
    half = genes // 2
    vmem = pl.BlockSpec(memory_space=pltpu.VMEM)
    held, sums, old = [], [], []
    for number, new in enumerate(STAGES):
        last = number == len(STAGES) - 1
        have = old + list(new)
        pairs = [p for p in PAIRS if max(p[:2]) in new]
        assert all(i in have and j in have for i, j, _ in pairs)
        args = [h for b in new for h in raw[b]] + held + sums
        x_shape = ((genes, S), jnp.bfloat16)
        out_shape = [jax.ShapeDtypeStruct((2, 16, half), jnp.float32)]
        if last:
            out_shape = [jax.ShapeDtypeStruct((2, half), jnp.float32)]
            out_shape += [jax.ShapeDtypeStruct((2, 8, half), jnp.float32)] * 2
        scratch = [
            pltpu.VMEM((len({j for _, j, both in pairs if both}), genes, 128), jnp.float32),
            pltpu.VMEM((len({i for i, _, _ in pairs}), 8, half), jnp.float32),
        ]
        if last:
            scratch = [pltpu.VMEM(*x_shape) for _ in new] + scratch
        else:
            out_shape += [jax.ShapeDtypeStruct(*x_shape) for _ in new]
        call = pl.pallas_call(
            functools.partial(stage_sums, tuple(old), new, tuple(pairs), last),
            out_shape=out_shape,
            in_specs=[vmem] * len(args),
            out_specs=[vmem] * len(out_shape),
            scratch_shapes=scratch,
            compiler_params=pltpu.CompilerParams(vmem_limit_bytes=VMEM_BYTES),
            cost_estimate=pl.CostEstimate(
                flops=len(pairs) * genes * genes * S, bytes_accessed=2**20, transcendentals=0
            ),
        )
        done = call(*args)
        sums = [done[0]]
        held += done[1:]
        old += new
    return done


def small(body, results):
    vmem = pl.BlockSpec(memory_space=pltpu.VMEM)
    return pl.pallas_call(
        body,
        out_shape=[jax.ShapeDtypeStruct(r.shape, r.dtype) for r in results],
        out_specs=[vmem] * len(results),
        compiler_params=pltpu.CompilerParams(vmem_limit_bytes=2**20),
    )


def on_device(expression):
    genes, _ = expression.shape
    got = {DELTA[0]: expression}
    for d, parent in OFFSETS[1:]:
        source = expression if parent is None else got[parent]
        got[d] = fetch(source, d if parent is None else minus(d, parent))
    raw = []
    for d in DELTA:
        raw.append((got[d], fetch(got[d], (0, 0, 0), 1)))
    own, keep, give = all_sums(raw, genes)
    got = fetch(give, (0, 0, 0), 1)
    joined = small(joined_sums, [own] * 5)(keep, got)
    arrived = [deliver(v, DELTA[1 + m], DELTA[6 + m]) for m, v in enumerate(joined)]
    mine, other = small(owner_sums, [own[:1]] * 2)(own, *arrived)
    return (mine + fetch(other, (0, 0, 0), 1)).reshape(genes // 2) - 1.0


def solution(mesh):
    torus = Mesh(mesh.devices.reshape(2, N, N, 2, 2), ALL)

    return jax.shard_map(
        on_device, mesh=torus, in_specs=(P(CHIP, "layer"),), out_specs=P(ALL), check_vma=False
    )
```

profile of v0, /device:TPU:1, one launch (start us, length us, event | category | flops | bytes accessed | tf_op | source)
XLA Modules:
  0.0 80.6 jit_solution(7667873183186344981)
XLA Ops:
  0.0 4.5 %collective-permute-start.3 = (bf16[384,512]{1,0:T(8,128)(2,1)}, bf16[384,512]{1,0:T(8,128)(2,1)S(1)}, u32[]{:S(2)}, u32[]{:S(2)}) collective-permute-start(bf16[384,512]{1,0:T(8,128)(2,1)} %refs_0_.1), channel_id=1, source_target_pairs={{70,0},{71,1},{86,16},{87,17},{102,32},{103,33},{118,48},{119,49},... | collective-permute-start | bytes 1179656 | tf_op jit(solution)/shard_map/ppermute | solution.py:73
  4.5 4.9 %collective-permute-start = (bf16[384,512]{1,0:T(8,128)(2,1)}, bf16[384,512]{1,0:T(8,128)(2,1)S(1)}, u32[]{:S(2)}, u32[]{:S(2)}) collective-permute-start(bf16[384,512]{1,0:T(8,128)(2,1)} %refs_0_.1), channel_id=1, source_target_pairs={{18,0},{19,1},{34,16},{35,17},{50,32},{51,33},{2,48},{3,49},{22,4}... | collective-permute-start | bytes 1179656 | tf_op jit(solution)/shard_map/ppermute | solution.py:73
  9.4 1.2 %collective-permute-start.11 = (bf16[384,512]{1,0:T(8,128)(2,1)}, bf16[384,512]{1,0:T(8,128)(2,1)S(1)}, u32[]{:S(2)}, u32[]{:S(2)}) collective-permute-start(bf16[384,512]{1,0:T(8,128)(2,1)} %refs_0_.1), channel_id=1, source_target_pairs={{1,0},{0,1},{17,16},{16,17},{33,32},{32,33},{49,48},{48,49},{5,4},... | collective-permute-start | bytes 1179656 | tf_op jit(solution)/shard_map/ppermute | solution.py:73
  10.7 2.4 %collective-permute-done.3.refs_4_ = bf16[384,512]{1,0:T(8,128)(2,1)S(1)} collective-permute-done((bf16[384,512]{1,0:T(8,128)(2,1)}, bf16[384,512]{1,0:T(8,128)(2,1)S(1)}, u32[]{:S(2)}, u32[]{:S(2)}) %collective-permute-start.3) | collective-permute-done | bytes 393248 | tf_op jit(solution)/shard_map/ppermute | solution.py:73
  13.1 3.8 %collective-permute-start.17 = (bf16[384,512]{1,0:T(8,128)(2,1)}, bf16[384,512]{1,0:T(8,128)(2,1)S(1)}, u32[]{:S(2)}, u32[]{:S(2)}) collective-permute-start(bf16[384,512]{1,0:T(8,128)(2,1)} %refs_0_.1), channel_id=1, source_target_pairs={{16,0},{17,1},{32,16},{33,17},{48,32},{49,33},{0,48},{1,49},{20,4}... | collective-permute-start | bytes 1179656 | tf_op jit(solution)/shard_map/ppermute | solution.py:73
  16.9 0.4 collective-permute-done.refs_2_
  17.3 0.2 collective-permute-start.19
  17.4 5.0 %collective-permute-done.6.refs_6_ = bf16[384,512]{1,0:T(8,128)(2,1)S(1)} collective-permute-done((bf16[384,512]{1,0:T(8,128)(2,1)}, bf16[384,512]{1,0:T(8,128)(2,1)S(1)}, u32[]{:S(2)}, u32[]{:S(2)}) %collective-permute-start.6) | collective-permute-done | bytes 393248 | tf_op jit(solution)/shard_map/ppermute | solution.py:73
  22.4 3.8 %collective-permute-start.13 = (bf16[384,512]{1,0:T(8,128)(2,1)S(1)}, bf16[384,512]{1,0:T(8,128)(2,1)S(1)}, u32[]{:S(2)}, u32[]{:S(2)}) collective-permute-start(bf16[384,512]{1,0:T(8,128)(2,1)S(1)} %collective-permute-done.3.refs_4_), channel_id=1, source_target_pairs={{1,0},{0,1},{17,16},{16,17},{33,32},{32,33},{49,48},{48,49},{5,4},... | collective-permute-start | bytes 1179656 | tf_op jit(solution)/shard_map/ppermute | solution.py:73
  26.2 0.6 collective-permute-done.15.refs_0_
  26.8 1.8 %collective-permute-start.14 = (bf16[384,512]{1,0:T(8,128)(2,1)S(1)}, bf16[384,512]{1,0:T(8,128)(2,1)S(1)}, u32[]{:S(2)}, u32[]{:S(2)}) collective-permute-start(bf16[384,512]{1,0:T(8,128)(2,1)S(1)} %collective-permute-done.6.refs_6_), channel_id=1, source_target_pairs={{1,0},{0,1},{17,16},{16,17},{33,32},{32,33},{49,48},{48,49},{5,4},... | collective-permute-start | bytes 1179656 | tf_op jit(solution)/shard_map/ppermute | solution.py:73
  28.6 3.2 %collective-permute-done.19.refs_4_ = bf16[384,512]{1,0:T(8,128)(2,1)S(1)} collective-permute-done((bf16[384,512]{1,0:T(8,128)(2,1)}, bf16[384,512]{1,0:T(8,128)(2,1)S(1)}, u32[]{:S(2)}, u32[]{:S(2)}) %collective-permute-start.19) | collective-permute-done | bytes 393248 | tf_op jit(solution)/shard_map/ppermute | solution.py:73
  31.8 1.1 %collective-permute-start.18 = (bf16[384,512]{1,0:T(8,128)(2,1)S(1)}, bf16[384,512]{1,0:T(8,128)(2,1)S(1)}, u32[]{:S(2)}, u32[]{:S(2)}) collective-permute-start(bf16[384,512]{1,0:T(8,128)(2,1)S(1)} %collective-permute-done.17.refs_2_), channel_id=1, source_target_pairs={{1,0},{0,1},{17,16},{16,17},{33,32},{32,33},{49,48},{48,49},{5,4},... | collective-permute-start | bytes 1179656 | tf_op jit(solution)/shard_map/ppermute | solution.py:73
  32.9 0.3 collective-permute-start.4
  33.3 2.4 %collective-permute-start.1 = (bf16[384,512]{1,0:T(8,128)(2,1)S(1)}, bf16[384,512]{1,0:T(8,128)(2,1)S(1)}, u32[]{:S(2)}, u32[]{:S(2)}) collective-permute-start(bf16[384,512]{1,0:T(8,128)(2,1)S(1)} %collective-permute-done.refs_2_), channel_id=1, source_target_pairs={{2,0},{3,1},{18,16},{19,17},{34,32},{35,33},{50,48},{51,49},{6,4},... | collective-permute-start | bytes 1179656 | tf_op jit(solution)/shard_map/ppermute | solution.py:73
  35.7 0.7 collective-permute-start.20
  36.3 8.5 %collective-permute-done.9.refs_6_ = bf16[384,512]{1,0:T(8,128)(2,1)S(1)} collective-permute-done((bf16[384,512]{1,0:T(8,128)(2,1)S(1)}, bf16[384,512]{1,0:T(8,128)(2,1)S(1)}, u32[]{:S(2)}, u32[]{:S(2)}) %collective-permute-start.9) | collective-permute-done | bytes 393248 | tf_op jit(solution)/shard_map/ppermute | solution.py:73
  44.8 0.9 %collective-permute-start.10 = (bf16[384,512]{1,0:T(8,128)(2,1)S(1)}, bf16[384,512]{1,0:T(8,128)(2,1)S(1)}, u32[]{:S(2)}, u32[]{:S(2)}) collective-permute-start(bf16[384,512]{1,0:T(8,128)(2,1)S(1)} %collective-permute-done.9.refs_6_), channel_id=1, source_target_pairs={{1,0},{0,1},{17,16},{16,17},{33,32},{32,33},{49,48},{48,49},{5,4},... | collective-permute-start | bytes 1179656 | tf_op jit(solution)/shard_map/ppermute | solution.py:73
  45.7 0.4 collective-permute-start.2
  46.2 0.8 %collective-permute-done.7.refs_4_ = bf16[384,512]{1,0:T(8,128)(2,1)S(1)} collective-permute-done((bf16[384,512]{1,0:T(8,128)(2,1)S(1)}, bf16[384,512]{1,0:T(8,128)(2,1)S(1)}, u32[]{:S(2)}, u32[]{:S(2)}) %collective-permute-start.7) | collective-permute-done | bytes 393248 | tf_op jit(solution)/shard_map/ppermute | solution.py:73
  47.0 1.4 %collective-permute-start.8 = (bf16[384,512]{1,0:T(8,128)(2,1)S(1)}, bf16[384,512]{1,0:T(8,128)(2,1)S(1)}, u32[]{:S(2)}, u32[]{:S(2)}) collective-permute-start(bf16[384,512]{1,0:T(8,128)(2,1)S(1)} %collective-permute-done.7.refs_4_), channel_id=1, source_target_pairs={{1,0},{0,1},{17,16},{16,17},{33,32},{32,33},{49,48},{48,49},{5,4},... | collective-permute-start | bytes 1179656 | tf_op jit(solution)/shard_map/ppermute | solution.py:73
  48.4 1.0 %copy-done = bf16[384,512]{1,0:T(8,128)(2,1)S(1)} copy-done((bf16[384,512]{1,0:T(8,128)(2,1)S(1)}, bf16[384,512]{1,0:T(8,128)(2,1)}, u32[]{:S(2)}) %copy-start) | copy-done | bytes 393240
  49.4 3.8 %shard_map.17 = (f32[2,16,192]{2,1,0:T(8,128)S(1)}, bf16[384,1024]{1,0:T(8,128)(2,1)S(1)}, bf16[384,1024]{1,0:T(8,128)(2,1)S(1)}, bf16[384,1024]{1,0:T(8,128)(2,1)S(1)}, bf16[384,1024]{1,0:T(8,128)(2,1)S(1)}) custom-call(bf16[384,512]{1,0:T(8,128)(2,1)S(1)} %copy-done, bf16[384,512]{1,0:T(8,128)(2,1)S(1)} %collective-permute-done.11.refs_1_, ...), custom_call_target="tpu_custom_call" | custom-call | flops 1056964608 | bytes 1048576 | tf_op jit(solution)/shard_map/pallas_call | solution.py:231
  53.2 4.3 %shard_map.18 = (f32[2,16,192]{2,1,0:T(8,128)S(1)}, bf16[384,1024]{1,0:T(8,128)(2,1)S(1)}, bf16[384,1024]{1,0:T(8,128)(2,1)S(1)}, bf16[384,1024]{1,0:T(8,128)(2,1)S(1)}) custom-call(bf16[384,512]{1,0:T(8,128)(2,1)S(1)} %collective-permute-done.15.refs_0_, bf16[384,512]{1,0:T(8,128)(2,1)S(1)} %collective-permute-done.16.refs_1_, ...), custom_call_target="tpu_custom_call" | custom-call | flops 1660944384 | bytes 1048576 | tf_op jit(solution)/shard_map/pallas_call | solution.py:231
  57.5 6.2 %shard_map.19 = (f32[2,192]{1,0:T(2,128)S(1)}, f32[2,8,192]{2,1,0:T(8,128)S(1)}, f32[2,8,192]{2,1,0:T(8,128)S(1)}) custom-call(bf16[384,512]{1,0:T(8,128)(2,1)S(1)} %collective-permute-done.1.refs_0_, bf16[384,512]{1,0:T(8,128)(2,1)S(1)} %collective-permute-done.2.refs_1_, bf16[384,512]{1,0:T(8,128)(2,1)S(1)} %collective-permute-done.4.refs_2_, ...), custom_call_target="tpu_custom_call" | custom-call | flops 2717908992 | bytes 1048576 | tf_op jit(solution)/shard_map/pallas_call | solution.py:231
  63.8 1.2 %collective-permute-done.21.got_ref = f32[2,8,192]{2,1,0:T(8,128)S(1)} collective-permute-done((f32[2,8,192]{2,1,0:T(8,128)S(1)}, f32[2,8,192]{2,1,0:T(8,128)S(1)}, u32[]{:S(2)}, u32[]{:S(2)}) %collective-permute-start.21) | collective-permute-done | bytes 12320 | tf_op jit(solution)/shard_map/ppermute | solution.py:73
  65.0 2.7 %collective-permute-start.22 = (f32[2,192]{1,0:T(2,128)S(1)}, f32[2,192]{1,0:T(2,128)S(1)}, u32[]{:S(2)}, u32[]{:S(2)}) collective-permute-start(f32[2,192]{1,0:T(2,128)S(1)} %get-tuple-element.36), channel_id=1, source_target_pairs={{0,18},{1,49},{16,34},{17,1},{32,50},{33,17},{48,2},{49,33},{4,22}... | collective-permute-start | bytes 4616 | tf_op jit(solution)/shard_map/ppermute | solution.py:82
  67.7 5.6 %collective-permute-start.25 = (f32[2,192]{1,0:T(2,128)S(1)}, f32[2,192]{1,0:T(2,128)S(1)}, u32[]{:S(2)}, u32[]{:S(2)}) collective-permute-start(f32[2,192]{1,0:T(2,128)S(1)} %get-tuple-element.39), channel_id=1, source_target_pairs={{0,12},{1,57},{16,28},{17,9},{32,44},{33,25},{48,60},{49,41},{4,0}... | collective-permute-start | bytes 4616 | tf_op jit(solution)/shard_map/ppermute | solution.py:82
  73.3 1.1 %collective-permute-start.26 = (f32[2,192]{1,0:T(2,128)S(1)}, f32[2,192]{1,0:T(2,128)S(1)}, u32[]{:S(2)}, u32[]{:S(2)}) collective-permute-start(f32[2,192]{1,0:T(2,128)S(1)} %get-tuple-element.40), channel_id=1, source_target_pairs={{0,16},{1,119},{16,32},{17,71},{32,48},{33,87},{48,0},{49,103},{4,... | collective-permute-start | bytes 4616 | tf_op jit(solution)/shard_map/ppermute | solution.py:82
  74.4 4.3 %collective-permute-done.26.refs_4_ = f32[2,192]{1,0:T(2,128)S(1)} collective-permute-done((f32[2,192]{1,0:T(2,128)S(1)}, f32[2,192]{1,0:T(2,128)S(1)}, u32[]{:S(2)}, u32[]{:S(2)}) %collective-permute-start.26) | collective-permute-done | bytes 1568 | tf_op jit(solution)/shard_map/ppermute | solution.py:82
  78.9 1.1 %collective-permute-done.27 = f32[1,192]{1,0:T(1,128)S(1)} collective-permute-done((f32[1,192]{1,0:T(1,128)S(1)}, f32[1,192]{1,0:T(1,128)S(1)}, u32[]{:S(2)}, u32[]{:S(2)}) %collective-permute-start.27) | collective-permute-done | bytes 800 | tf_op jit(solution)/shard_map/ppermute | solution.py:73
  80.0 0.6 add_add_fusion
  (32 shorter events, 0.3 us)
Async XLA Ops:
  0.0 13.1 %collective-permute-start.3 = (bf16[384,512]{1,0:T(8,128)(2,1)}, bf16[384,512]{1,0:T(8,128)(2,1)S(1)}, u32[]{:S(2)}, u32[]{:S(2)}) collective-permute-start(bf16[384,512]{1,0:T(8,128)(2,1)} %refs_0_.1), channel_id=1, source_target_pairs={{70,0},{71,1},{86,16},{87,17},{102,32},{103,33},{118,48},{119,49},... | collective-permute-start | bytes 1179656 | tf_op jit(solution)/shard_map/ppermute | solution.py:73
  4.5 12.8 %collective-permute-start = (bf16[384,512]{1,0:T(8,128)(2,1)}, bf16[384,512]{1,0:T(8,128)(2,1)S(1)}, u32[]{:S(2)}, u32[]{:S(2)}) collective-permute-start(bf16[384,512]{1,0:T(8,128)(2,1)} %refs_0_.1), channel_id=1, source_target_pairs={{18,0},{19,1},{34,16},{35,17},{50,32},{51,33},{2,48},{3,49},{22,4}... | collective-permute-start | bytes 1179656 | tf_op jit(solution)/shard_map/ppermute | solution.py:73
  9.4 13.0 %collective-permute-start.6 = (bf16[384,512]{1,0:T(8,128)(2,1)}, bf16[384,512]{1,0:T(8,128)(2,1)S(1)}, u32[]{:S(2)}, u32[]{:S(2)}) collective-permute-start(bf16[384,512]{1,0:T(8,128)(2,1)} %refs_0_.1), channel_id=1, source_target_pairs={{60,0},{61,1},{12,16},{13,17},{28,32},{29,33},{44,48},{45,49},{48,... | collective-permute-start | bytes 1179656 | tf_op jit(solution)/shard_map/ppermute | solution.py:73
  9.4 16.8 %collective-permute-start.11 = (bf16[384,512]{1,0:T(8,128)(2,1)}, bf16[384,512]{1,0:T(8,128)(2,1)S(1)}, u32[]{:S(2)}, u32[]{:S(2)}) collective-permute-start(bf16[384,512]{1,0:T(8,128)(2,1)} %refs_0_.1), channel_id=1, source_target_pairs={{1,0},{0,1},{17,16},{16,17},{33,32},{32,33},{49,48},{48,49},{5,4},... | collective-permute-start | bytes 1179656 | tf_op jit(solution)/shard_map/ppermute | solution.py:73
  10.7 16.2 %collective-permute-start.15 = (bf16[384,512]{1,0:T(8,128)(2,1)}, bf16[384,512]{1,0:T(8,128)(2,1)S(1)}, u32[]{:S(2)}, u32[]{:S(2)}) collective-permute-start(bf16[384,512]{1,0:T(8,128)(2,1)} %refs_0_.1), channel_id=1, source_target_pairs={{12,0},{13,1},{28,16},{29,17},{44,32},{45,33},{60,48},{61,49},{0,4... | collective-permute-start | bytes 1179656 | tf_op jit(solution)/shard_map/ppermute | solution.py:73
  13.1 15.5 %collective-permute-start.17 = (bf16[384,512]{1,0:T(8,128)(2,1)}, bf16[384,512]{1,0:T(8,128)(2,1)S(1)}, u32[]{:S(2)}, u32[]{:S(2)}) collective-permute-start(bf16[384,512]{1,0:T(8,128)(2,1)} %refs_0_.1), channel_id=1, source_target_pairs={{16,0},{17,1},{32,16},{33,17},{48,32},{49,33},{0,48},{1,49},{20,4}... | collective-permute-start | bytes 1179656 | tf_op jit(solution)/shard_map/ppermute | solution.py:73
  17.3 14.5 %collective-permute-start.19 = (bf16[384,512]{1,0:T(8,128)(2,1)}, bf16[384,512]{1,0:T(8,128)(2,1)S(1)}, u32[]{:S(2)}, u32[]{:S(2)}) collective-permute-start(bf16[384,512]{1,0:T(8,128)(2,1)} %refs_0_.1), channel_id=1, source_target_pairs={{48,0},{49,1},{0,16},{1,17},{16,32},{17,33},{32,48},{33,49},{52,4}... | collective-permute-start | bytes 1179656 | tf_op jit(solution)/shard_map/ppermute | solution.py:73
  22.4 10.5 %collective-permute-start.13 = (bf16[384,512]{1,0:T(8,128)(2,1)S(1)}, bf16[384,512]{1,0:T(8,128)(2,1)S(1)}, u32[]{:S(2)}, u32[]{:S(2)}) collective-permute-start(bf16[384,512]{1,0:T(8,128)(2,1)S(1)} %collective-permute-done.3.refs_4_), channel_id=1, source_target_pairs={{1,0},{0,1},{17,16},{16,17},{33,32},{32,33},{49,48},{48,49},{5,4},... | collective-permute-start | bytes 1179656 | tf_op jit(solution)/shard_map/ppermute | solution.py:73
  26.2 6.7 %collective-permute-start.12 = (bf16[384,512]{1,0:T(8,128)(2,1)S(1)}, bf16[384,512]{1,0:T(8,128)(2,1)S(1)}, u32[]{:S(2)}, u32[]{:S(2)}) collective-permute-start(bf16[384,512]{1,0:T(8,128)(2,1)S(1)} %collective-permute-done.refs_2_), channel_id=1, source_target_pairs={{1,0},{0,1},{17,16},{16,17},{33,32},{32,33},{49,48},{48,49},{5,4},... | collective-permute-start | bytes 1179656 | tf_op jit(solution)/shard_map/ppermute | solution.py:73
  26.8 6.5 %collective-permute-start.14 = (bf16[384,512]{1,0:T(8,128)(2,1)S(1)}, bf16[384,512]{1,0:T(8,128)(2,1)S(1)}, u32[]{:S(2)}, u32[]{:S(2)}) collective-permute-start(bf16[384,512]{1,0:T(8,128)(2,1)S(1)} %collective-permute-done.6.refs_6_), channel_id=1, source_target_pairs={{1,0},{0,1},{17,16},{16,17},{33,32},{32,33},{49,48},{48,49},{5,4},... | collective-permute-start | bytes 1179656 | tf_op jit(solution)/shard_map/ppermute | solution.py:73
  28.6 7.0 %collective-permute-start.16 = (bf16[384,512]{1,0:T(8,128)(2,1)S(1)}, bf16[384,512]{1,0:T(8,128)(2,1)S(1)}, u32[]{:S(2)}, u32[]{:S(2)}) collective-permute-start(bf16[384,512]{1,0:T(8,128)(2,1)S(1)} %collective-permute-done.15.refs_0_), channel_id=1, source_target_pairs={{1,0},{0,1},{17,16},{16,17},{33,32},{32,33},{49,48},{48,49},{5,4},... | collective-permute-start | bytes 1179656 | tf_op jit(solution)/shard_map/ppermute | solution.py:73
  31.8 3.9 %collective-permute-start.18 = (bf16[384,512]{1,0:T(8,128)(2,1)S(1)}, bf16[384,512]{1,0:T(8,128)(2,1)S(1)}, u32[]{:S(2)}, u32[]{:S(2)}) collective-permute-start(bf16[384,512]{1,0:T(8,128)(2,1)S(1)} %collective-permute-done.17.refs_2_), channel_id=1, source_target_pairs={{1,0},{0,1},{17,16},{16,17},{33,32},{32,33},{49,48},{48,49},{5,4},... | collective-permute-start | bytes 1179656 | tf_op jit(solution)/shard_map/ppermute | solution.py:73
  32.9 11.9 %collective-permute-start.9 = (bf16[384,512]{1,0:T(8,128)(2,1)S(1)}, bf16[384,512]{1,0:T(8,128)(2,1)S(1)}, u32[]{:S(2)}, u32[]{:S(2)}) collective-permute-start(bf16[384,512]{1,0:T(8,128)(2,1)S(1)} %collective-permute-done.3.refs_4_), channel_id=1, source_target_pairs={{48,0},{49,1},{0,16},{1,17},{16,32},{17,33},{32,48},{33,49},{52,4}... | collective-permute-start | bytes 1179656 | tf_op jit(solution)/shard_map/ppermute | solution.py:73
  32.9 12.7 %collective-permute-start.4 = (bf16[384,512]{1,0:T(8,128)(2,1)S(1)}, bf16[384,512]{1,0:T(8,128)(2,1)S(1)}, u32[]{:S(2)}, u32[]{:S(2)}) collective-permute-start(bf16[384,512]{1,0:T(8,128)(2,1)S(1)} %collective-permute-done.3.refs_4_), channel_id=1, source_target_pairs={{66,0},{67,1},{82,16},{83,17},{98,32},{99,33},{114,48},{115,49},{7... | collective-permute-start | bytes 1179656 | tf_op jit(solution)/shard_map/ppermute | solution.py:73
  33.3 12.5 %collective-permute-start.1 = (bf16[384,512]{1,0:T(8,128)(2,1)S(1)}, bf16[384,512]{1,0:T(8,128)(2,1)S(1)}, u32[]{:S(2)}, u32[]{:S(2)}) collective-permute-start(bf16[384,512]{1,0:T(8,128)(2,1)S(1)} %collective-permute-done.refs_2_), channel_id=1, source_target_pairs={{2,0},{3,1},{18,16},{19,17},{34,32},{35,33},{50,48},{51,49},{6,4},... | collective-permute-start | bytes 1179656 | tf_op jit(solution)/shard_map/ppermute | solution.py:73
  35.7 11.3 %collective-permute-start.7 = (bf16[384,512]{1,0:T(8,128)(2,1)S(1)}, bf16[384,512]{1,0:T(8,128)(2,1)S(1)}, u32[]{:S(2)}, u32[]{:S(2)}) collective-permute-start(bf16[384,512]{1,0:T(8,128)(2,1)S(1)} %collective-permute-done.6.refs_6_), channel_id=1, source_target_pairs={{12,0},{13,1},{28,16},{29,17},{44,32},{45,33},{60,48},{61,49},{0,4... | collective-permute-start | bytes 1179656 | tf_op jit(solution)/shard_map/ppermute | solution.py:73
  35.7 17.5 %collective-permute-start.20 = (bf16[384,512]{1,0:T(8,128)(2,1)S(1)}, bf16[384,512]{1,0:T(8,128)(2,1)S(1)}, u32[]{:S(2)}, u32[]{:S(2)}) collective-permute-start(bf16[384,512]{1,0:T(8,128)(2,1)S(1)} %collective-permute-done.19.refs_4_), channel_id=1, source_target_pairs={{1,0},{0,1},{17,16},{16,17},{33,32},{32,33},{49,48},{48,49},{5,4},... | collective-permute-start | bytes 1179656 | tf_op jit(solution)/shard_map/ppermute | solution.py:73
  44.8 12.7 %collective-permute-start.10 = (bf16[384,512]{1,0:T(8,128)(2,1)S(1)}, bf16[384,512]{1,0:T(8,128)(2,1)S(1)}, u32[]{:S(2)}, u32[]{:S(2)}) collective-permute-start(bf16[384,512]{1,0:T(8,128)(2,1)S(1)} %collective-permute-done.9.refs_6_), channel_id=1, source_target_pairs={{1,0},{0,1},{17,16},{16,17},{33,32},{32,33},{49,48},{48,49},{5,4},... | collective-permute-start | bytes 1179656 | tf_op jit(solution)/shard_map/ppermute | solution.py:73
  45.7 11.9 %collective-permute-start.5 = (bf16[384,512]{1,0:T(8,128)(2,1)S(1)}, bf16[384,512]{1,0:T(8,128)(2,1)S(1)}, u32[]{:S(2)}, u32[]{:S(2)}) collective-permute-start(bf16[384,512]{1,0:T(8,128)(2,1)S(1)} %collective-permute-done.4.refs_2_), channel_id=1, source_target_pairs={{1,0},{0,1},{17,16},{16,17},{33,32},{32,33},{49,48},{48,49},{5,4},... | collective-permute-start | bytes 1179656 | tf_op jit(solution)/shard_map/ppermute | solution.py:73
  45.7 11.8 %collective-permute-start.2 = (bf16[384,512]{1,0:T(8,128)(2,1)S(1)}, bf16[384,512]{1,0:T(8,128)(2,1)S(1)}, u32[]{:S(2)}, u32[]{:S(2)}) collective-permute-start(bf16[384,512]{1,0:T(8,128)(2,1)S(1)} %collective-permute-done.1.refs_0_), channel_id=1, source_target_pairs={{1,0},{0,1},{17,16},{16,17},{33,32},{32,33},{49,48},{48,49},{5,4},... | collective-permute-start | bytes 1179656 | tf_op jit(solution)/shard_map/ppermute | solution.py:73
  47.0 10.6 %collective-permute-start.8 = (bf16[384,512]{1,0:T(8,128)(2,1)S(1)}, bf16[384,512]{1,0:T(8,128)(2,1)S(1)}, u32[]{:S(2)}, u32[]{:S(2)}) collective-permute-start(bf16[384,512]{1,0:T(8,128)(2,1)S(1)} %collective-permute-done.7.refs_4_), channel_id=1, source_target_pairs={{1,0},{0,1},{17,16},{16,17},{33,32},{32,33},{49,48},{48,49},{5,4},... | collective-permute-start | bytes 1179656 | tf_op jit(solution)/shard_map/ppermute | solution.py:73
  48.4 1.0 %copy-start = (bf16[384,512]{1,0:T(8,128)(2,1)S(1)}, bf16[384,512]{1,0:T(8,128)(2,1)}, u32[]{:S(2)}) copy-start(bf16[384,512]{1,0:T(8,128)(2,1)} %refs_0_.1) | copy-start | bytes 1179652
  63.7 1.2 %collective-permute-start.21 = (f32[2,8,192]{2,1,0:T(8,128)S(1)}, f32[2,8,192]{2,1,0:T(8,128)S(1)}, u32[]{:S(2)}, u32[]{:S(2)}) collective-permute-start(f32[2,8,192]{2,1,0:T(8,128)S(1)} %get-tuple-element.35), channel_id=1, source_target_pairs={{1,0},{0,1},{17,16},{16,17},{33,32},{32,33},{49,48},{48,49},{5,4},... | collective-permute-start | bytes 36872 | tf_op jit(solution)/shard_map/ppermute | solution.py:73
  65.0 9.5 %collective-permute-start.22 = (f32[2,192]{1,0:T(2,128)S(1)}, f32[2,192]{1,0:T(2,128)S(1)}, u32[]{:S(2)}, u32[]{:S(2)}) collective-permute-start(f32[2,192]{1,0:T(2,128)S(1)} %get-tuple-element.36), channel_id=1, source_target_pairs={{0,18},{1,49},{16,34},{17,1},{32,50},{33,17},{48,2},{49,33},{4,22}... | collective-permute-start | bytes 4616 | tf_op jit(solution)/shard_map/ppermute | solution.py:82
  67.6 6.8 %collective-permute-start.23 = (f32[2,192]{1,0:T(2,128)S(1)}, f32[2,192]{1,0:T(2,128)S(1)}, u32[]{:S(2)}, u32[]{:S(2)}) collective-permute-start(f32[2,192]{1,0:T(2,128)S(1)} %get-tuple-element.37), channel_id=1, source_target_pairs={{0,70},{1,81},{16,86},{17,97},{32,102},{33,113},{48,118},{49,65},{... | collective-permute-start | bytes 4616 | tf_op jit(solution)/shard_map/ppermute | solution.py:82
  67.6 6.8 %collective-permute-start.24 = (f32[2,192]{1,0:T(2,128)S(1)}, f32[2,192]{1,0:T(2,128)S(1)}, u32[]{:S(2)}, u32[]{:S(2)}) collective-permute-start(f32[2,192]{1,0:T(2,128)S(1)} %get-tuple-element.38), channel_id=1, source_target_pairs={{0,60},{1,69},{16,12},{17,85},{32,28},{33,101},{48,44},{49,117},{4... | collective-permute-start | bytes 4616 | tf_op jit(solution)/shard_map/ppermute | solution.py:82
  67.7 6.7 %collective-permute-start.25 = (f32[2,192]{1,0:T(2,128)S(1)}, f32[2,192]{1,0:T(2,128)S(1)}, u32[]{:S(2)}, u32[]{:S(2)}) collective-permute-start(f32[2,192]{1,0:T(2,128)S(1)} %get-tuple-element.39), channel_id=1, source_target_pairs={{0,12},{1,57},{16,28},{17,9},{32,44},{33,25},{48,60},{49,41},{4,0}... | collective-permute-start | bytes 4616 | tf_op jit(solution)/shard_map/ppermute | solution.py:82
  73.3 5.4 %collective-permute-start.26 = (f32[2,192]{1,0:T(2,128)S(1)}, f32[2,192]{1,0:T(2,128)S(1)}, u32[]{:S(2)}, u32[]{:S(2)}) collective-permute-start(f32[2,192]{1,0:T(2,128)S(1)} %get-tuple-element.40), channel_id=1, source_target_pairs={{0,16},{1,119},{16,32},{17,71},{32,48},{33,87},{48,0},{49,103},{4,... | collective-permute-start | bytes 4616 | tf_op jit(solution)/shard_map/ppermute | solution.py:82
  78.8 1.2 %collective-permute-start.27 = (f32[1,192]{1,0:T(1,128)S(1)}, f32[1,192]{1,0:T(1,128)S(1)}, u32[]{:S(2)}, u32[]{:S(2)}) collective-permute-start(f32[1,192]{1,0:T(1,128)S(1)} %get-tuple-element.42), channel_id=1, source_target_pairs={{1,0},{0,1},{17,16},{16,17},{33,32},{32,33},{49,48},{48,49},{5,4},... | collective-permute-start | bytes 2312 | tf_op jit(solution)/shard_map/ppermute | solution.py:73
where the time goes:
time: 80.7 us; the launch traced here: 80.6 us
  starting transfers between devices  37.1 us (46%)
  waiting for transfers between devices  27.5 us (34%)
  Pallas kernels  14.3 us (18%)
  local copies, waits for them, and re-layouts  1 us (1%)
    ppermute x23, starting transfers between devices, fetch(): return lax.ppermute(value, ALL, pairs)  27.7 us
    ppermute x23, waiting for transfers between devices, fetch(): return lax.ppermute(value, ALL, pairs)  23.2 us
    pallas_call x3, Pallas kernels, all_sums(): done = call(*args)  14.3 us
    ppermute x5, starting transfers between devices, deliver(): return lax.ppermute(value, ALL, pairs)  9.46 us
    ppermute x5, waiting for transfers between devices, deliver(): return lax.ppermute(value, ALL, pairs)  4.34 us
  transfers between devices with their start and end apart: 28, of which 10 were waited for; matrix products, arithmetic and copies ran while one was open for 0% of the time, Pallas kernels for 10%

commit v1 on v0

v1 whole, which is shorter than its diff:
```python
import functools
import itertools

import jax
import jax.numpy as jnp
from jax import lax
from jax.experimental import pallas as pl
from jax.experimental.pallas import tpu as pltpu
from jax.sharding import Mesh
from jax.sharding import PartitionSpec as P


S = 1024
N = 4
CHIP = ("x_hi", "z", "y", "x_lo")
ALL = CHIP + ("layer",)
epsilon = 1e-05
VMEM_BYTES = 16 * 2**20


OFFSETS = (
    ((0, 0, 0), None),
    ((1, 0, 3), None),
    ((3, 1, 0), None),
    ((0, 0, 1), None),
    ((0, 3, 0), None),
    ((2, 0, 3), (1, 0, 3)),
    ((2, 1, 0), (3, 1, 0)),
    ((3, 1, 3), (3, 1, 0)),
    ((0, 1, 0), None),
    ((0, 3, 1), (0, 0, 1)),
    ((0, 3, 2), (0, 3, 0)),
)
DELTA = tuple(d for d, _ in OFFSETS)
BLOCKS = len(DELTA)


def minus(a, b):
    return tuple((p - q) % N for p, q in zip(a, b))


def choose_pairs():
    pairs, done = [(0, 0, False)], {(0, 0, 0)}
    for j, i in itertools.product(range(BLOCKS), range(BLOCKS)):
        if i >= j:
            continue
        d = minus(DELTA[i], DELTA[j])
        if d not in done:
            e = minus((0, 0, 0), d)
            done |= {d, e}
            pairs.append((i, j, d != e))
    assert len(done) == N**3
    return tuple(pairs)


PAIRS = choose_pairs()


def place(x, y, z, c):
    return (((x // 2 * N + z) * N + y) * 2 + x % 2) * 2 + c


def chips():
    return itertools.product(range(N), range(N), range(N))


def fetch(value, d, flip=0):
    pairs = []
    for p in chips():
        q = tuple((a + b) % N for a, b in zip(p, d))
        for c in range(2):
            pairs.append((place(*q, c ^ flip), place(*p, c)))
    return lax.ppermute(value, ALL, pairs)


def deliver(value, d0, d1):
    pairs = []
    for p in chips():
        for c, d in enumerate((d0, d1)):
            q = tuple((a + b) % N for a, b in zip(p, d))
            pairs.append((place(*p, c), place(*q, c)))
    return lax.ppermute(value, ALL, pairs)


def standardize(own_ref, other_ref, own_out, other_out):
    rows = 32
    for r in range(0, own_ref.shape[0], rows):
        here = pl.ds(r, rows)
        own = own_ref[here, :].astype(jnp.float32)
        other = other_ref[here, :].astype(jnp.float32)
        total = jnp.sum(own, axis=1, keepdims=True) + jnp.sum(other, axis=1, keepdims=True)
        squares = jnp.sum(own * own, axis=1, keepdims=True) + jnp.sum(
            other * other, axis=1, keepdims=True
        )
        average = total / S
        variance = squares / S - average * average
        scale = lax.rsqrt(variance + epsilon)
        own_out[here, :] = (((own - average) * scale) * 0.03125).astype(jnp.bfloat16)
        other_out[here, :] = (((other - average) * scale) * 0.03125).astype(jnp.bfloat16)


def runs_of(pairs, order):
    found = []
    for j, both in sorted({(j, both) for _, j, both in pairs}):
        places = sorted(order.index(i) for i, q, t in pairs if (q, t) == (j, both))
        for place in places:
            if found and found[-1][0] == j and found[-1][2] == both and found[-1][1][-1] == place - 1:
                found[-1][1].append(place)
            else:
                found.append((j, [place], both))
    return found


def stage_sums(blocks, pairs, first, last, *refs):
    refs = list(refs)
    held = {b: (refs.pop(0), refs.pop(0)) for b in blocks}
    before = None if first else refs.pop(0)
    if last:
        own_ref, keep_ref, give_ref = refs.pop(0), refs.pop(0), refs.pop(0)
    else:
        out_ref = refs.pop(0)
    row_ref, col_ref, right0_ref, right1_ref = refs
    core = lax.axis_index("layer")
    genes = held[blocks[0]][0].shape[0]
    half = genes // 2
    mine = pl.ds(pl.multiple_of(core * half, half), half)
    order = sorted({i for i, _, _ in pairs})
    for place, i in enumerate(order):
        for right_ref, block_ref in zip((right0_ref, right1_ref), held[i]):
            right_ref[place * half : (place + 1) * half, :] = block_ref[mine, :]
    rows_of = sorted({j for _, j, both in pairs if both})
    begun = set()
    for j, places, both in runs_of(pairs, order):
        wide = pl.ds(places[0] * half, len(places) * half)
        t = sum(
            lax.dot_general(
                left_ref[...],
                right_ref[wide, :],
                (((1,), (1,)), ((), ())),
                preferred_element_type=jnp.float32,
            )
            for left_ref, right_ref in zip(held[j], (right0_ref, right1_ref))
        )
        t = 1.0 + t
        t = t * t
        t = t * t
        t = t * t * t
        cols = jnp.sum(t.reshape(genes // 8, 8, t.shape[1]), axis=0)
        for k, place in enumerate(places):
            part = cols[:, k * half : (k + 1) * half]
            if ("c", place) in begun:
                col_ref[place] += part
            else:
                col_ref[place] = part
                begun.add(("c", place))
        if both:
            r = rows_of.index(j)
            full = t.shape[1] // 128 * 128
            part = sum(t[:, q : q + 128] for q in range(0, full, 128))
            if ("r", j) in begun:
                row_ref[r] += part
            else:
                row_ref[r] = part
                begun.add(("r", j))
            if full < t.shape[1]:
                row_ref[r, :, : t.shape[1] - full] += t[:, full:]
    ones = jnp.ones((8, 128), jnp.float32)
    for b in range(BLOCKS):
        parts = [jnp.zeros((1, half), jnp.float32)] * 2
        if before is not None:
            parts = [before[h, pl.ds(b, 1), :] for h in range(2)]
        if b in rows_of:
            rows = lax.dot_general(
                ones,
                row_ref[rows_of.index(b)],
                (((1,), (1,)), ((), ())),
                precision=lax.Precision.HIGHEST,
                preferred_element_type=jnp.float32,
            )
            parts = [p + rows[:1, h * half : (h + 1) * half] for h, p in enumerate(parts)]
        if b in order:
            cols = jnp.sum(col_ref[order.index(b)], axis=0, keepdims=True)
            parts = [p + jnp.where(core == h, cols, 0.0) for h, p in enumerate(parts)]
        for h in range(2):
            if not last:
                out_ref[h, pl.ds(b, 1), :] = parts[h]
            elif b == 0:
                own_ref[pl.ds(h, 1), :] = parts[h] * (0.5**12)
            else:
                kept = jnp.where(core == (b - 1) // 5, 1.0, 0.0) * (0.5**12)
                row = pl.ds((b - 1) % 5, 1)
                if b <= 5:
                    keep_ref[h, row, :] = parts[h] * kept
                    give_ref[h, row, :] = parts[h] * (0.5**12 - kept)
                else:
                    keep_ref[h, row, :] += parts[h] * kept
                    give_ref[h, row, :] += parts[h] * (0.5**12 - kept)


def joined_sums(keep_ref, got_ref, *out_refs):
    for m, out_ref in enumerate(out_refs):
        for h in range(2):
            row = pl.ds(m, 1)
            out_ref[pl.ds(h, 1), :] = keep_ref[h, row, :] + got_ref[h, row, :]


def owner_sums(own_ref, *refs):
    *arrived, mine_ref, other_ref = refs
    total = own_ref[...]
    for ref in arrived:
        total += ref[...]
    first = lax.axis_index("layer") == 0
    mine_ref[...] = jnp.where(first, total[:1], total[1:])
    other_ref[...] = jnp.where(first, total[1:], total[:1])


STAGES = ((0, 1, 2, 3, 4), (5, 6, 7), (8, 9, 10))


def all_sums(held, genes):
    half = genes // 2
    vmem = pl.BlockSpec(memory_space=pltpu.VMEM)
    done = []
    for number, new in enumerate(STAGES):
        first, last = number == 0, number == len(STAGES) - 1
        pairs = [p for p in PAIRS if max(p[:2]) in new]
        blocks = sorted({b for p in pairs for b in p[:2]})
        args = [h for b in blocks for h in held[b]] + done
        out_shape = [jax.ShapeDtypeStruct((2, 16, half), jnp.float32)]
        if last:
            out_shape = [jax.ShapeDtypeStruct((2, half), jnp.float32)]
            out_shape += [jax.ShapeDtypeStruct((2, 8, half), jnp.float32)] * 2
        right = len({i for i, _, _ in pairs})
        call = pl.pallas_call(
            functools.partial(stage_sums, tuple(blocks), tuple(pairs), first, last),
            out_shape=out_shape,
            in_specs=[vmem] * len(args),
            out_specs=[vmem] * len(out_shape),
            scratch_shapes=[
                pltpu.VMEM((len({j for _, j, both in pairs if both}), genes, 128), jnp.float32),
                pltpu.VMEM((right, 8, half), jnp.float32),
                pltpu.VMEM((right * half, S // 2), jnp.bfloat16),
                pltpu.VMEM((right * half, S // 2), jnp.bfloat16),
            ],
            compiler_params=pltpu.CompilerParams(vmem_limit_bytes=VMEM_BYTES),
            cost_estimate=pl.CostEstimate(
                flops=len(pairs) * genes * genes * S, bytes_accessed=2**20, transcendentals=0
            ),
        )
        done = list(call(*args))
    return done


def small(body, results, limit=2**20):
    vmem = pl.BlockSpec(memory_space=pltpu.VMEM)
    return pl.pallas_call(
        body,
        out_shape=[jax.ShapeDtypeStruct(r.shape, r.dtype) for r in results],
        out_specs=[vmem] * len(results),
        compiler_params=pltpu.CompilerParams(vmem_limit_bytes=limit),
    )


def on_device(expression):
    genes, _ = expression.shape
    other = fetch(expression, (0, 0, 0), 1)
    held = [small(standardize, [expression] * 2, 8 * 2**20)(expression, other)]
    got = {DELTA[0]: held[0][0]}
    for b, (d, parent) in enumerate(OFFSETS):
        if b == 0:
            continue
        source = DELTA[0] if parent is None else parent
        got[d] = fetch(got[source], minus(d, source))
        held.append((got[d], fetch(got[d], (0, 0, 0), 1)))
    own, keep, give = all_sums(held, genes)
    got = fetch(give, (0, 0, 0), 1)
    joined = small(joined_sums, [own] * 5)(keep, got)
    arrived = [deliver(v, DELTA[1 + m], DELTA[6 + m]) for m, v in enumerate(joined)]
    mine, other = small(owner_sums, [own[:1]] * 2)(own, *arrived)
    return (mine + fetch(other, (0, 0, 0), 1)).reshape(genes // 2) - 1.0


def solution(mesh):
    torus = Mesh(mesh.devices.reshape(2, N, N, 2, 2), ALL)

    return jax.shard_map(
        on_device, mesh=torus, in_specs=(P(CHIP, "layer"),), out_specs=P(ALL), check_vma=False
    )
```

time: 80.7 us -> 80.5 us (level)
  Pallas kernels: 14.3 us -> 10.4 us
  waiting for transfers between devices: 27.5 us -> 30.2 us
  starting transfers between devices: 37.1 us -> 38.1 us
    pallas_call x3 -> x4, Pallas kernels: 14.3 us -> 10.4 us  [the longest x3 9.95 us: all_sums(): done = list(call(*args))]
    ppermute x23, waiting for transfers between devices: 23.2 us -> 25.4 us  [fetch(): return lax.ppermute(value, ALL, pairs)]
    ppermute x23, starting transfers between devices: 27.7 us -> 29.3 us  [fetch(): return lax.ppermute(value, ALL, pairs)]
  transfers between devices with their start and end apart: 28 -> 28, of which waited for: 10 -> 11; matrix products, arithmetic and copies ran while one was open for 0% -> 0% of each run, Pallas kernels for 10% -> 8%
where the time goes in v1:
time: 80.5 us; the launch traced here: 80.3 us
  starting transfers between devices  38.1 us (47%)
  waiting for transfers between devices  30.2 us (38%)
  Pallas kernels  10.4 us (13%)
  local copies, waits for them, and re-layouts  1 us (1%)
    ppermute x23, starting transfers between devices, fetch(): return lax.ppermute(value, ALL, pairs)  29.3 us
    ppermute x23, waiting for transfers between devices, fetch(): return lax.ppermute(value, ALL, pairs)  25.4 us
    pallas_call x3, Pallas kernels, all_sums(): done = list(call(*args))  9.95 us
    ppermute x5, starting transfers between devices, deliver(): return lax.ppermute(value, ALL, pairs)  8.86 us
    ppermute x5, waiting for transfers between devices, deliver(): return lax.ppermute(value, ALL, pairs)  4.82 us
  transfers between devices with their start and end apart: 28, of which 11 were waited for; matrix products, arithmetic and copies ran while one was open for 0% of the time, Pallas kernels for 8%

profile of v1, /device:TPU:1, one launch (start us, length us, event | category | flops | bytes accessed | tf_op | source)
XLA Modules:
  0.0 80.3 jit_solution(6392525752432123471)
XLA Ops:
  0.0 1.4 %collective-permute-start = (bf16[384,512]{1,0:T(8,128)(2,1)}, bf16[384,512]{1,0:T(8,128)(2,1)S(1)}, u32[]{:S(2)}, u32[]{:S(2)}) collective-permute-start(bf16[384,512]{1,0:T(8,128)(2,1)} %own_ref.1), channel_id=1, source_target_pairs={{1,0},{0,1},{17,16},{16,17},{33,32},{32,33},{49,48},{48,49},{5,4},... | collective-permute-start | bytes 1179656 | tf_op jit(solution)/shard_map/ppermute | solution.py:73
  1.4 1.6 %collective-permute-done.other_ref = bf16[384,512]{1,0:T(8,128)(2,1)S(1)} collective-permute-done((bf16[384,512]{1,0:T(8,128)(2,1)}, bf16[384,512]{1,0:T(8,128)(2,1)S(1)}, u32[]{:S(2)}, u32[]{:S(2)}) %collective-permute-start) | collective-permute-done | bytes 393248 | tf_op jit(solution)/shard_map/ppermute | solution.py:73
  2.9 1.0 %copy-done = bf16[384,512]{1,0:T(8,128)(2,1)S(1)} copy-done((bf16[384,512]{1,0:T(8,128)(2,1)S(1)}, bf16[384,512]{1,0:T(8,128)(2,1)}, u32[]{:S(2)}) %copy-start) | copy-done | bytes 393240
  4.4 4.0 %collective-permute-start.1 = (bf16[384,512]{1,0:T(8,128)(2,1)S(1)}, bf16[384,512]{1,0:T(8,128)(2,1)S(1)}, u32[]{:S(2)}, u32[]{:S(2)}) collective-permute-start(bf16[384,512]{1,0:T(8,128)(2,1)S(1)} %get-tuple-element.17.refs_0_), channel_id=1, source_target_pairs={{50,0},{51,1},{2,16},{3,17},{18,32},{19,33},{34,48},{35,49},{54,4}... | collective-permute-start | bytes 1179656 | tf_op jit(solution)/shard_map/ppermute | solution.py:73
  8.4 1.0 %collective-permute-start.3 = (bf16[384,512]{1,0:T(8,128)(2,1)S(1)}, bf16[384,512]{1,0:T(8,128)(2,1)S(1)}, u32[]{:S(2)}, u32[]{:S(2)}) collective-permute-start(bf16[384,512]{1,0:T(8,128)(2,1)S(1)} %get-tuple-element.17.refs_0_), channel_id=1, source_target_pairs={{16,0},{17,1},{32,16},{33,17},{48,32},{49,33},{0,48},{1,49},{20,4}... | collective-permute-start | bytes 1179656 | tf_op jit(solution)/shard_map/ppermute | solution.py:73
  9.4 1.3 %collective-permute-start.5 = (bf16[384,512]{1,0:T(8,128)(2,1)S(1)}, bf16[384,512]{1,0:T(8,128)(2,1)S(1)}, u32[]{:S(2)}, u32[]{:S(2)}) collective-permute-start(bf16[384,512]{1,0:T(8,128)(2,1)S(1)} %get-tuple-element.17.refs_0_), channel_id=1, source_target_pairs={{12,0},{13,1},{28,16},{29,17},{44,32},{45,33},{60,48},{61,49},{0,4... | collective-permute-start | bytes 1179656 | tf_op jit(solution)/shard_map/ppermute | solution.py:73
  10.7 1.3 %collective-permute-start.9 = (bf16[384,512]{1,0:T(8,128)(2,1)S(1)}, bf16[384,512]{1,0:T(8,128)(2,1)S(1)}, u32[]{:S(2)}, u32[]{:S(2)}) collective-permute-start(bf16[384,512]{1,0:T(8,128)(2,1)S(1)} %get-tuple-element.17.refs_0_), channel_id=1, source_target_pairs={{70,0},{71,1},{86,16},{87,17},{102,32},{103,33},{118,48},{119,49},... | collective-permute-start | bytes 1179656 | tf_op jit(solution)/shard_map/ppermute | solution.py:73
  12.1 1.5 %collective-permute-start.14 = (bf16[384,512]{1,0:T(8,128)(2,1)S(1)}, bf16[384,512]{1,0:T(8,128)(2,1)S(1)}, u32[]{:S(2)}, u32[]{:S(2)}) collective-permute-start(bf16[384,512]{1,0:T(8,128)(2,1)S(1)} %get-tuple-element.17.refs_0_), channel_id=1, source_target_pairs={{4,0},{5,1},{20,16},{21,17},{36,32},{37,33},{52,48},{53,49},{8,4},... | collective-permute-start | bytes 1179656 | tf_op jit(solution)/shard_map/ppermute | solution.py:73
  13.5 4.8 %collective-permute-done.1.refs_2_ = bf16[384,512]{1,0:T(8,128)(2,1)S(1)} collective-permute-done((bf16[384,512]{1,0:T(8,128)(2,1)S(1)}, bf16[384,512]{1,0:T(8,128)(2,1)S(1)}, u32[]{:S(2)}, u32[]{:S(2)}) %collective-permute-start.1) | collective-permute-done | bytes 393248 | tf_op jit(solution)/shard_map/ppermute | solution.py:73
  18.4 0.9 %collective-permute-start.2 = (bf16[384,512]{1,0:T(8,128)(2,1)S(1)}, bf16[384,512]{1,0:T(8,128)(2,1)S(1)}, u32[]{:S(2)}, u32[]{:S(2)}) collective-permute-start(bf16[384,512]{1,0:T(8,128)(2,1)S(1)} %collective-permute-done.1.refs_2_), channel_id=1, source_target_pairs={{1,0},{0,1},{17,16},{16,17},{33,32},{32,33},{49,48},{48,49},{5,4},... | collective-permute-start | bytes 1179656 | tf_op jit(solution)/shard_map/ppermute | solution.py:73
  19.3 0.8 collective-permute-start.4
  20.5 1.7 %collective-permute-start.6 = (bf16[384,512]{1,0:T(8,128)(2,1)S(1)}, bf16[384,512]{1,0:T(8,128)(2,1)S(1)}, u32[]{:S(2)}, u32[]{:S(2)}) collective-permute-start(bf16[384,512]{1,0:T(8,128)(2,1)S(1)} %collective-permute-done.5.refs_8_.refs_6_), channel_id=1, source_target_pairs={{1,0},{0,1},{17,16},{16,17},{33,32},{32,33},{49,48},{48,49},{5,4},... | collective-permute-start | bytes 1179656 | tf_op jit(solution)/shard_map/ppermute | solution.py:73
  22.3 2.1 %collective-permute-start.20 = (bf16[384,512]{1,0:T(8,128)(2,1)S(1)}, bf16[384,512]{1,0:T(8,128)(2,1)S(1)}, u32[]{:S(2)}, u32[]{:S(2)}) collective-permute-start(bf16[384,512]{1,0:T(8,128)(2,1)S(1)} %collective-permute-done.9.refs_4_), channel_id=1, source_target_pairs={{1,0},{0,1},{17,16},{16,17},{33,32},{32,33},{49,48},{48,49},{5,4},... | collective-permute-start | bytes 1179656 | tf_op jit(solution)/shard_map/ppermute | solution.py:73
  24.5 6.3 %collective-permute-done.14.refs_14_ = bf16[384,512]{1,0:T(8,128)(2,1)S(1)} collective-permute-done((bf16[384,512]{1,0:T(8,128)(2,1)S(1)}, bf16[384,512]{1,0:T(8,128)(2,1)S(1)}, u32[]{:S(2)}, u32[]{:S(2)}) %collective-permute-start.14) | collective-permute-done | bytes 393248 | tf_op jit(solution)/shard_map/ppermute | solution.py:73
  31.8 1.7 %collective-permute-start.7 = (bf16[384,512]{1,0:T(8,128)(2,1)S(1)}, bf16[384,512]{1,0:T(8,128)(2,1)S(1)}, u32[]{:S(2)}, u32[]{:S(2)}) collective-permute-start(bf16[384,512]{1,0:T(8,128)(2,1)S(1)} %collective-permute-done.1.refs_2_), channel_id=1, source_target_pairs={{2,0},{3,1},{18,16},{19,17},{34,32},{35,33},{50,48},{51,49},{6,4},... | collective-permute-start | bytes 1179656 | tf_op jit(solution)/shard_map/ppermute | solution.py:73
  33.9 2.7 %collective-permute-start.18 = (bf16[384,512]{1,0:T(8,128)(2,1)S(1)}, bf16[384,512]{1,0:T(8,128)(2,1)S(1)}, u32[]{:S(2)}, u32[]{:S(2)}) collective-permute-start(bf16[384,512]{1,0:T(8,128)(2,1)S(1)} %collective-permute-done.5.refs_8_.refs_6_), channel_id=1, source_target_pairs={{32,0},{33,1},{48,16},{49,17},{0,32},{1,33},{16,48},{17,49},{36,4}... | collective-permute-start | bytes 1179656 | tf_op jit(solution)/shard_map/ppermute | solution.py:73
  36.7 4.7 %collective-permute-done.10.refs_12_.refs_10_ = bf16[384,512]{1,0:T(8,128)(2,1)S(1)} collective-permute-done((bf16[384,512]{1,0:T(8,128)(2,1)S(1)}, bf16[384,512]{1,0:T(8,128)(2,1)S(1)}, u32[]{:S(2)}, u32[]{:S(2)}) %collective-permute-start.10) | collective-permute-done | bytes 393248 | tf_op jit(solution)/shard_map/ppermute | solution.py:73
  41.4 2.1 %collective-permute-start.11 = (bf16[384,512]{1,0:T(8,128)(2,1)S(1)}, bf16[384,512]{1,0:T(8,128)(2,1)S(1)}, u32[]{:S(2)}, u32[]{:S(2)}) collective-permute-start(bf16[384,512]{1,0:T(8,128)(2,1)S(1)} %collective-permute-done.10.refs_12_.refs_10_), channel_id=1, source_target_pairs={{1,0},{0,1},{17,16},{16,17},{33,32},{32,33},{49,48},{48,49},{5,4},... | collective-permute-start | bytes 1179656 | tf_op jit(solution)/shard_map/ppermute | solution.py:73
  43.5 0.8 collective-permute-start.13
  44.3 2.0 %collective-permute-start.15 = (bf16[384,512]{1,0:T(8,128)(2,1)S(1)}, bf16[384,512]{1,0:T(8,128)(2,1)S(1)}, u32[]{:S(2)}, u32[]{:S(2)}) collective-permute-start(bf16[384,512]{1,0:T(8,128)(2,1)S(1)} %collective-permute-done.14.refs_14_), channel_id=1, source_target_pairs={{1,0},{0,1},{17,16},{16,17},{33,32},{32,33},{49,48},{48,49},{5,4},... | collective-permute-start | bytes 1179656 | tf_op jit(solution)/shard_map/ppermute | solution.py:73
  46.3 5.5 %collective-permute-done.18.refs_18_ = bf16[384,512]{1,0:T(8,128)(2,1)S(1)} collective-permute-done((bf16[384,512]{1,0:T(8,128)(2,1)S(1)}, bf16[384,512]{1,0:T(8,128)(2,1)S(1)}, u32[]{:S(2)}, u32[]{:S(2)}) %collective-permute-start.18) | collective-permute-done | bytes 393248 | tf_op jit(solution)/shard_map/ppermute | solution.py:73
  51.8 1.6 %collective-permute-start.17 = (bf16[384,512]{1,0:T(8,128)(2,1)S(1)}, bf16[384,512]{1,0:T(8,128)(2,1)S(1)}, u32[]{:S(2)}, u32[]{:S(2)}) collective-permute-start(bf16[384,512]{1,0:T(8,128)(2,1)S(1)} %collective-permute-done.16.refs_16_), channel_id=1, source_target_pairs={{1,0},{0,1},{17,16},{16,17},{33,32},{32,33},{49,48},{48,49},{5,4},... | collective-permute-start | bytes 1179656 | tf_op jit(solution)/shard_map/ppermute | solution.py:73
  53.4 3.1 %shard_map.18.refs_16_ = f32[2,16,192]{2,1,0:T(8,128)S(1)} custom-call(bf16[384,512]{1,0:T(8,128)(2,1)S(1)} %get-tuple-element.17.refs_0_, bf16[384,512]{1,0:T(8,128)(2,1)S(1)} %get-tuple-element.18.refs_1_, bf16[384,512]{1,0:T(8,128)(2,1)S(1)} %collective-permute-done.1.refs_2_, bf16[384,512]{1,0:T(8,128)(2,1)S(1)} %collective-permute-done.2.refs_3_, ...), custom_call_target="tpu_custom_call" | custom-call | flops 1660944384 | bytes 1048576 | tf_op jit(solution)/shard_map/pallas_call | solution.py:250
  56.5 3.0 %shard_map.19.refs_20_ = f32[2,16,192]{2,1,0:T(8,128)S(1)} custom-call(bf16[384,512]{1,0:T(8,128)(2,1)S(1)} %get-tuple-element.17.refs_0_, bf16[384,512]{1,0:T(8,128)(2,1)S(1)} %get-tuple-element.18.refs_1_, bf16[384,512]{1,0:T(8,128)(2,1)S(1)} %collective-permute-done.1.refs_2_, bf16[384,512]{1,0:T(8,128)(2,1)S(1)} %collective-permute-done.2.refs_3_, ...), custom_call_target="tpu_custom_call" | custom-call | flops 1509949440 | bytes 1048576 | tf_op jit(solution)/shard_map/pallas_call | solution.py:250
  59.5 3.9 %shard_map.20 = (f32[2,192]{1,0:T(2,128)S(1)}, f32[2,8,192]{2,1,0:T(8,128)S(1)}, f32[2,8,192]{2,1,0:T(8,128)S(1)}) custom-call(bf16[384,512]{1,0:T(8,128)(2,1)S(1)} %get-tuple-element.17.refs_0_, bf16[384,512]{1,0:T(8,128)(2,1)S(1)} %get-tuple-element.18.refs_1_, bf16[384,512]{1,0:T(8,128)(2,1)S(1)} %collective-permute-done.1.refs_2_, ...), custom_call_target="tpu_custom_call" | custom-call | flops 2264924160 | bytes 1048576 | tf_op jit(solution)/shard_map/pallas_call | solution.py:250
  64.0 0.8 %collective-permute-done.21.got_ref = f32[2,8,192]{2,1,0:T(8,128)S(1)} collective-permute-done((f32[2,8,192]{2,1,0:T(8,128)S(1)}, f32[2,8,192]{2,1,0:T(8,128)S(1)}, u32[]{:S(2)}, u32[]{:S(2)}) %collective-permute-start.21) | collective-permute-done | bytes 12320 | tf_op jit(solution)/shard_map/ppermute | solution.py:73
  64.8 2.7 %collective-permute-start.22 = (f32[2,192]{1,0:T(2,128)S(1)}, f32[2,192]{1,0:T(2,128)S(1)}, u32[]{:S(2)}, u32[]{:S(2)}) collective-permute-start(f32[2,192]{1,0:T(2,128)S(1)} %get-tuple-element.22), channel_id=1, source_target_pairs={{0,50},{1,69},{16,2},{17,85},{32,18},{33,101},{48,34},{49,117},{4,... | collective-permute-start | bytes 4616 | tf_op jit(solution)/shard_map/ppermute | solution.py:82
  67.5 1.0 %collective-permute-start.24 = (f32[2,192]{1,0:T(2,128)S(1)}, f32[2,192]{1,0:T(2,128)S(1)}, u32[]{:S(2)}, u32[]{:S(2)}) collective-permute-start(f32[2,192]{1,0:T(2,128)S(1)} %get-tuple-element.24), channel_id=1, source_target_pairs={{0,16},{1,5},{16,32},{17,21},{32,48},{33,37},{48,0},{49,53},{4,20}... | collective-permute-start | bytes 4616 | tf_op jit(solution)/shard_map/ppermute | solution.py:82
  68.5 5.2 %collective-permute-start.25 = (f32[2,192]{1,0:T(2,128)S(1)}, f32[2,192]{1,0:T(2,128)S(1)}, u32[]{:S(2)}, u32[]{:S(2)}) collective-permute-start(f32[2,192]{1,0:T(2,128)S(1)} %get-tuple-element.25), channel_id=1, source_target_pairs={{0,12},{1,29},{16,28},{17,45},{32,44},{33,61},{48,60},{49,13},{4,0... | collective-permute-start | bytes 4616 | tf_op jit(solution)/shard_map/ppermute | solution.py:82
  73.7 0.7 collective-permute-done.25.refs_3_
  74.4 4.1 %collective-permute-done.26.refs_4_ = f32[2,192]{1,0:T(2,128)S(1)} collective-permute-done((f32[2,192]{1,0:T(2,128)S(1)}, f32[2,192]{1,0:T(2,128)S(1)}, u32[]{:S(2)}, u32[]{:S(2)}) %collective-permute-start.26) | collective-permute-done | bytes 1568 | tf_op jit(solution)/shard_map/ppermute | solution.py:82
  78.7 1.1 %collective-permute-done.27 = f32[1,192]{1,0:T(1,128)S(1)} collective-permute-done((f32[1,192]{1,0:T(1,128)S(1)}, f32[1,192]{1,0:T(1,128)S(1)}, u32[]{:S(2)}, u32[]{:S(2)}) %collective-permute-start.27) | collective-permute-done | bytes 800 | tf_op jit(solution)/shard_map/ppermute | solution.py:73
  (33 shorter events, 3.8 us)
Async XLA Ops:
  0.0 2.9 %collective-permute-start = (bf16[384,512]{1,0:T(8,128)(2,1)}, bf16[384,512]{1,0:T(8,128)(2,1)S(1)}, u32[]{:S(2)}, u32[]{:S(2)}) collective-permute-start(bf16[384,512]{1,0:T(8,128)(2,1)} %own_ref.1), channel_id=1, source_target_pairs={{1,0},{0,1},{17,16},{16,17},{33,32},{32,33},{49,48},{48,49},{5,4},... | collective-permute-start | bytes 1179656 | tf_op jit(solution)/shard_map/ppermute | solution.py:73
  2.9 1.0 %copy-start = (bf16[384,512]{1,0:T(8,128)(2,1)S(1)}, bf16[384,512]{1,0:T(8,128)(2,1)}, u32[]{:S(2)}) copy-start(bf16[384,512]{1,0:T(8,128)(2,1)} %own_ref.1) | copy-start | bytes 1179652
  4.4 14.0 %collective-permute-start.1 = (bf16[384,512]{1,0:T(8,128)(2,1)S(1)}, bf16[384,512]{1,0:T(8,128)(2,1)S(1)}, u32[]{:S(2)}, u32[]{:S(2)}) collective-permute-start(bf16[384,512]{1,0:T(8,128)(2,1)S(1)} %get-tuple-element.17.refs_0_), channel_id=1, source_target_pairs={{50,0},{51,1},{2,16},{3,17},{18,32},{19,33},{34,48},{35,49},{54,4}... | collective-permute-start | bytes 1179656 | tf_op jit(solution)/shard_map/ppermute | solution.py:73
  8.4 10.9 %collective-permute-start.3 = (bf16[384,512]{1,0:T(8,128)(2,1)S(1)}, bf16[384,512]{1,0:T(8,128)(2,1)S(1)}, u32[]{:S(2)}, u32[]{:S(2)}) collective-permute-start(bf16[384,512]{1,0:T(8,128)(2,1)S(1)} %get-tuple-element.17.refs_0_), channel_id=1, source_target_pairs={{16,0},{17,1},{32,16},{33,17},{48,32},{49,33},{0,48},{1,49},{20,4}... | collective-permute-start | bytes 1179656 | tf_op jit(solution)/shard_map/ppermute | solution.py:73
  9.4 11.1 %collective-permute-start.5 = (bf16[384,512]{1,0:T(8,128)(2,1)S(1)}, bf16[384,512]{1,0:T(8,128)(2,1)S(1)}, u32[]{:S(2)}, u32[]{:S(2)}) collective-permute-start(bf16[384,512]{1,0:T(8,128)(2,1)S(1)} %get-tuple-element.17.refs_0_), channel_id=1, source_target_pairs={{12,0},{13,1},{28,16},{29,17},{44,32},{45,33},{60,48},{61,49},{0,4... | collective-permute-start | bytes 1179656 | tf_op jit(solution)/shard_map/ppermute | solution.py:73
  10.7 11.6 %collective-permute-start.9 = (bf16[384,512]{1,0:T(8,128)(2,1)S(1)}, bf16[384,512]{1,0:T(8,128)(2,1)S(1)}, u32[]{:S(2)}, u32[]{:S(2)}) collective-permute-start(bf16[384,512]{1,0:T(8,128)(2,1)S(1)} %get-tuple-element.17.refs_0_), channel_id=1, source_target_pairs={{70,0},{71,1},{86,16},{87,17},{102,32},{103,33},{118,48},{119,49},... | collective-permute-start | bytes 1179656 | tf_op jit(solution)/shard_map/ppermute | solution.py:73
  12.1 18.7 %collective-permute-start.14 = (bf16[384,512]{1,0:T(8,128)(2,1)S(1)}, bf16[384,512]{1,0:T(8,128)(2,1)S(1)}, u32[]{:S(2)}, u32[]{:S(2)}) collective-permute-start(bf16[384,512]{1,0:T(8,128)(2,1)S(1)} %get-tuple-element.17.refs_0_), channel_id=1, source_target_pairs={{4,0},{5,1},{20,16},{21,17},{36,32},{37,33},{52,48},{53,49},{8,4},... | collective-permute-start | bytes 1179656 | tf_op jit(solution)/shard_map/ppermute | solution.py:73
  18.4 12.9 %collective-permute-start.2 = (bf16[384,512]{1,0:T(8,128)(2,1)S(1)}, bf16[384,512]{1,0:T(8,128)(2,1)S(1)}, u32[]{:S(2)}, u32[]{:S(2)}) collective-permute-start(bf16[384,512]{1,0:T(8,128)(2,1)S(1)} %collective-permute-done.1.refs_2_), channel_id=1, source_target_pairs={{1,0},{0,1},{17,16},{16,17},{33,32},{32,33},{49,48},{48,49},{5,4},... | collective-permute-start | bytes 1179656 | tf_op jit(solution)/shard_map/ppermute | solution.py:73
  19.3 12.5 %collective-permute-start.4 = (bf16[384,512]{1,0:T(8,128)(2,1)S(1)}, bf16[384,512]{1,0:T(8,128)(2,1)S(1)}, u32[]{:S(2)}, u32[]{:S(2)}) collective-permute-start(bf16[384,512]{1,0:T(8,128)(2,1)S(1)} %collective-permute-done.3.refs_6_.refs_4_), channel_id=1, source_target_pairs={{1,0},{0,1},{17,16},{16,17},{33,32},{32,33},{49,48},{48,49},{5,4},... | collective-permute-start | bytes 1179656 | tf_op jit(solution)/shard_map/ppermute | solution.py:73
  20.5 13.0 %collective-permute-start.6 = (bf16[384,512]{1,0:T(8,128)(2,1)S(1)}, bf16[384,512]{1,0:T(8,128)(2,1)S(1)}, u32[]{:S(2)}, u32[]{:S(2)}) collective-permute-start(bf16[384,512]{1,0:T(8,128)(2,1)S(1)} %collective-permute-done.5.refs_8_.refs_6_), channel_id=1, source_target_pairs={{1,0},{0,1},{17,16},{16,17},{33,32},{32,33},{49,48},{48,49},{5,4},... | collective-permute-start | bytes 1179656 | tf_op jit(solution)/shard_map/ppermute | solution.py:73
  22.3 11.6 %collective-permute-start.20 = (bf16[384,512]{1,0:T(8,128)(2,1)S(1)}, bf16[384,512]{1,0:T(8,128)(2,1)S(1)}, u32[]{:S(2)}, u32[]{:S(2)}) collective-permute-start(bf16[384,512]{1,0:T(8,128)(2,1)S(1)} %collective-permute-done.9.refs_4_), channel_id=1, source_target_pairs={{1,0},{0,1},{17,16},{16,17},{33,32},{32,33},{49,48},{48,49},{5,4},... | collective-permute-start | bytes 1179656 | tf_op jit(solution)/shard_map/ppermute | solution.py:73
  30.7 10.6 %collective-permute-start.10 = (bf16[384,512]{1,0:T(8,128)(2,1)S(1)}, bf16[384,512]{1,0:T(8,128)(2,1)S(1)}, u32[]{:S(2)}, u32[]{:S(2)}) collective-permute-start(bf16[384,512]{1,0:T(8,128)(2,1)S(1)} %collective-permute-done.9.refs_4_), channel_id=1, source_target_pairs={{66,0},{67,1},{82,16},{83,17},{98,32},{99,33},{114,48},{115,49},{7... | collective-permute-start | bytes 1179656 | tf_op jit(solution)/shard_map/ppermute | solution.py:73
  31.3 12.2 %collective-permute-start.12 = (bf16[384,512]{1,0:T(8,128)(2,1)S(1)}, bf16[384,512]{1,0:T(8,128)(2,1)S(1)}, u32[]{:S(2)}, u32[]{:S(2)}) collective-permute-start(bf16[384,512]{1,0:T(8,128)(2,1)S(1)} %collective-permute-done.9.refs_4_), channel_id=1, source_target_pairs={{48,0},{49,1},{0,16},{1,17},{16,32},{17,33},{32,48},{33,49},{52,4}... | collective-permute-start | bytes 1179656 | tf_op jit(solution)/shard_map/ppermute | solution.py:73
  31.8 12.4 %collective-permute-start.7 = (bf16[384,512]{1,0:T(8,128)(2,1)S(1)}, bf16[384,512]{1,0:T(8,128)(2,1)S(1)}, u32[]{:S(2)}, u32[]{:S(2)}) collective-permute-start(bf16[384,512]{1,0:T(8,128)(2,1)S(1)} %collective-permute-done.1.refs_2_), channel_id=1, source_target_pairs={{2,0},{3,1},{18,16},{19,17},{34,32},{35,33},{50,48},{51,49},{6,4},... | collective-permute-start | bytes 1179656 | tf_op jit(solution)/shard_map/ppermute | solution.py:73
  33.5 10.8 %collective-permute-start.16 = (bf16[384,512]{1,0:T(8,128)(2,1)S(1)}, bf16[384,512]{1,0:T(8,128)(2,1)S(1)}, u32[]{:S(2)}, u32[]{:S(2)}) collective-permute-start(bf16[384,512]{1,0:T(8,128)(2,1)S(1)} %collective-permute-done.3.refs_6_.refs_4_), channel_id=1, source_target_pairs={{12,0},{13,1},{28,16},{29,17},{44,32},{45,33},{60,48},{61,49},{0,4... | collective-permute-start | bytes 1179656 | tf_op jit(solution)/shard_map/ppermute | solution.py:73
  33.9 17.9 %collective-permute-start.18 = (bf16[384,512]{1,0:T(8,128)(2,1)S(1)}, bf16[384,512]{1,0:T(8,128)(2,1)S(1)}, u32[]{:S(2)}, u32[]{:S(2)}) collective-permute-start(bf16[384,512]{1,0:T(8,128)(2,1)S(1)} %collective-permute-done.5.refs_8_.refs_6_), channel_id=1, source_target_pairs={{32,0},{33,1},{48,16},{49,17},{0,32},{1,33},{16,48},{17,49},{36,4}... | collective-permute-start | bytes 1179656 | tf_op jit(solution)/shard_map/ppermute | solution.py:73
  41.4 12.1 %collective-permute-start.11 = (bf16[384,512]{1,0:T(8,128)(2,1)S(1)}, bf16[384,512]{1,0:T(8,128)(2,1)S(1)}, u32[]{:S(2)}, u32[]{:S(2)}) collective-permute-start(bf16[384,512]{1,0:T(8,128)(2,1)S(1)} %collective-permute-done.10.refs_12_.refs_10_), channel_id=1, source_target_pairs={{1,0},{0,1},{17,16},{16,17},{33,32},{32,33},{49,48},{48,49},{5,4},... | collective-permute-start | bytes 1179656 | tf_op jit(solution)/shard_map/ppermute | solution.py:73
  43.5 13.0 %collective-permute-start.13 = (bf16[384,512]{1,0:T(8,128)(2,1)S(1)}, bf16[384,512]{1,0:T(8,128)(2,1)S(1)}, u32[]{:S(2)}, u32[]{:S(2)}) collective-permute-start(bf16[384,512]{1,0:T(8,128)(2,1)S(1)} %collective-permute-done.12.refs_14_.refs_12_), channel_id=1, source_target_pairs={{1,0},{0,1},{17,16},{16,17},{33,32},{32,33},{49,48},{48,49},{5,4},... | collective-permute-start | bytes 1179656 | tf_op jit(solution)/shard_map/ppermute | solution.py:73
  44.3 12.3 %collective-permute-start.8 = (bf16[384,512]{1,0:T(8,128)(2,1)S(1)}, bf16[384,512]{1,0:T(8,128)(2,1)S(1)}, u32[]{:S(2)}, u32[]{:S(2)}) collective-permute-start(bf16[384,512]{1,0:T(8,128)(2,1)S(1)} %collective-permute-done.7.refs_10_.refs_8_), channel_id=1, source_target_pairs={{1,0},{0,1},{17,16},{16,17},{33,32},{32,33},{49,48},{48,49},{5,4},... | collective-permute-start | bytes 1179656 | tf_op jit(solution)/shard_map/ppermute | solution.py:73
  44.3 15.2 %collective-permute-start.15 = (bf16[384,512]{1,0:T(8,128)(2,1)S(1)}, bf16[384,512]{1,0:T(8,128)(2,1)S(1)}, u32[]{:S(2)}, u32[]{:S(2)}) collective-permute-start(bf16[384,512]{1,0:T(8,128)(2,1)S(1)} %collective-permute-done.14.refs_14_), channel_id=1, source_target_pairs={{1,0},{0,1},{17,16},{16,17},{33,32},{32,33},{49,48},{48,49},{5,4},... | collective-permute-start | bytes 1179656 | tf_op jit(solution)/shard_map/ppermute | solution.py:73
  51.8 7.7 %collective-permute-start.17 = (bf16[384,512]{1,0:T(8,128)(2,1)S(1)}, bf16[384,512]{1,0:T(8,128)(2,1)S(1)}, u32[]{:S(2)}, u32[]{:S(2)}) collective-permute-start(bf16[384,512]{1,0:T(8,128)(2,1)S(1)} %collective-permute-done.16.refs_16_), channel_id=1, source_target_pairs={{1,0},{0,1},{17,16},{16,17},{33,32},{32,33},{49,48},{48,49},{5,4},... | collective-permute-start | bytes 1179656 | tf_op jit(solution)/shard_map/ppermute | solution.py:73
  53.4 6.1 %collective-permute-start.19 = (bf16[384,512]{1,0:T(8,128)(2,1)S(1)}, bf16[384,512]{1,0:T(8,128)(2,1)S(1)}, u32[]{:S(2)}, u32[]{:S(2)}) collective-permute-start(bf16[384,512]{1,0:T(8,128)(2,1)S(1)} %collective-permute-done.18.refs_18_), channel_id=1, source_target_pairs={{1,0},{0,1},{17,16},{16,17},{33,32},{32,33},{49,48},{48,49},{5,4},... | collective-permute-start | bytes 1179656 | tf_op jit(solution)/shard_map/ppermute | solution.py:73
  63.4 1.4 %collective-permute-start.21 = (f32[2,8,192]{2,1,0:T(8,128)S(1)}, f32[2,8,192]{2,1,0:T(8,128)S(1)}, u32[]{:S(2)}, u32[]{:S(2)}) collective-permute-start(f32[2,8,192]{2,1,0:T(8,128)S(1)} %get-tuple-element.21), channel_id=1, source_target_pairs={{1,0},{0,1},{17,16},{16,17},{33,32},{32,33},{49,48},{48,49},{5,4},... | collective-permute-start | bytes 36872 | tf_op jit(solution)/shard_map/ppermute | solution.py:73
  64.8 8.9 %collective-permute-start.22 = (f32[2,192]{1,0:T(2,128)S(1)}, f32[2,192]{1,0:T(2,128)S(1)}, u32[]{:S(2)}, u32[]{:S(2)}) collective-permute-start(f32[2,192]{1,0:T(2,128)S(1)} %get-tuple-element.22), channel_id=1, source_target_pairs={{0,50},{1,69},{16,2},{17,85},{32,18},{33,101},{48,34},{49,117},{4,... | collective-permute-start | bytes 4616 | tf_op jit(solution)/shard_map/ppermute | solution.py:82
  67.5 6.2 %collective-permute-start.23 = (f32[2,192]{1,0:T(2,128)S(1)}, f32[2,192]{1,0:T(2,128)S(1)}, u32[]{:S(2)}, u32[]{:S(2)}) collective-permute-start(f32[2,192]{1,0:T(2,128)S(1)} %get-tuple-element.23), channel_id=1, source_target_pairs={{0,70},{1,119},{16,86},{17,71},{32,102},{33,87},{48,118},{49,103},... | collective-permute-start | bytes 4616 | tf_op jit(solution)/shard_map/ppermute | solution.py:82
  67.5 6.2 %collective-permute-start.24 = (f32[2,192]{1,0:T(2,128)S(1)}, f32[2,192]{1,0:T(2,128)S(1)}, u32[]{:S(2)}, u32[]{:S(2)}) collective-permute-start(f32[2,192]{1,0:T(2,128)S(1)} %get-tuple-element.24), channel_id=1, source_target_pairs={{0,16},{1,5},{16,32},{17,21},{32,48},{33,37},{48,0},{49,53},{4,20}... | collective-permute-start | bytes 4616 | tf_op jit(solution)/shard_map/ppermute | solution.py:82
  68.5 5.9 %collective-permute-start.25 = (f32[2,192]{1,0:T(2,128)S(1)}, f32[2,192]{1,0:T(2,128)S(1)}, u32[]{:S(2)}, u32[]{:S(2)}) collective-permute-start(f32[2,192]{1,0:T(2,128)S(1)} %get-tuple-element.25), channel_id=1, source_target_pairs={{0,12},{1,29},{16,28},{17,45},{32,44},{33,61},{48,60},{49,13},{4,0... | collective-permute-start | bytes 4616 | tf_op jit(solution)/shard_map/ppermute | solution.py:82
  73.7 4.8 %collective-permute-start.26 = (f32[2,192]{1,0:T(2,128)S(1)}, f32[2,192]{1,0:T(2,128)S(1)}, u32[]{:S(2)}, u32[]{:S(2)}) collective-permute-start(f32[2,192]{1,0:T(2,128)S(1)} %get-tuple-element.26), channel_id=1, source_target_pairs={{0,112},{1,45},{16,64},{17,61},{32,80},{33,13},{48,96},{49,29},{4,... | collective-permute-start | bytes 4616 | tf_op jit(solution)/shard_map/ppermute | solution.py:82
  78.5 1.2 %collective-permute-start.27 = (f32[1,192]{1,0:T(1,128)S(1)}, f32[1,192]{1,0:T(1,128)S(1)}, u32[]{:S(2)}, u32[]{:S(2)}) collective-permute-start(f32[1,192]{1,0:T(1,128)S(1)} %get-tuple-element.28), channel_id=1, source_target_pairs={{1,0},{0,1},{17,16},{16,17},{33,32},{32,33},{49,48},{48,49},{5,4},... | collective-permute-start | bytes 2312 | tf_op jit(solution)/shard_map/ppermute | solution.py:73

commit v2 on v1

--- a/solution.py
+++ b/solution.py
@@ -20,17 +20,19 @@
 
 OFFSETS = (
     ((0, 0, 0), None),
+    ((0, 3, 0), None),
+    ((3, 1, 0), None),
     ((1, 0, 3), None),
-    ((3, 1, 0), None),
     ((0, 0, 1), None),
-    ((0, 3, 0), None),
+    ((0, 3, 2), (0, 3, 0)),
+    ((3, 1, 3), (3, 1, 0)),
     ((2, 0, 3), (1, 0, 3)),
     ((2, 1, 0), (3, 1, 0)),
-    ((3, 1, 3), (3, 1, 0)),
+    ((0, 3, 1), (0, 0, 1)),
     ((0, 1, 0), None),
-    ((0, 3, 1), (0, 0, 1)),
-    ((0, 3, 2), (0, 3, 0)),
 )
+STAGES = ((0, 1, 2, 3, 4), (7,), (8, 9), (10, 5), (6,))
+SENDS = ((6, 7), (5, 8), (2, 3), (9, 1), (4, 10))
 DELTA = tuple(d for d, _ in OFFSETS)
 BLOCKS = len(DELTA)
 
@@ -41,9 +43,8 @@
 
 def choose_pairs():
     pairs, done = [(0, 0, False)], {(0, 0, 0)}
-    for j, i in itertools.product(range(BLOCKS), range(BLOCKS)):
-        if i >= j:
-            continue
+    order = [b for new in STAGES for b in new]
+    for i, j in ((i, j) for k, j in enumerate(order) for i in order[:k]):
         d = minus(DELTA[i], DELTA[j])
         if d not in done:
             e = minus((0, 0, 0), d)
@@ -80,6 +81,10 @@
             q = tuple((a + b) % N for a, b in zip(p, d))
             pairs.append((place(*p, c), place(*q, c)))
     return lax.ppermute(value, ALL, pairs)
+
+
+def bring(in_ref, out_ref):
+    out_ref[...] = in_ref[...]
 
 
 def standardize(own_ref, other_ref, own_out, other_out):
@@ -165,6 +170,7 @@
             if full < t.shape[1]:
                 row_ref[r, :, : t.shape[1] - full] += t[:, full:]
     ones = jnp.ones((8, 128), jnp.float32)
+    late = []
     for b in range(BLOCKS):
         parts = [jnp.zeros((1, half), jnp.float32)] * 2
         if before is not None:
@@ -187,14 +193,18 @@
             elif b == 0:
                 own_ref[pl.ds(h, 1), :] = parts[h] * (0.5**12)
             else:
-                kept = jnp.where(core == (b - 1) // 5, 1.0, 0.0) * (0.5**12)
-                row = pl.ds((b - 1) % 5, 1)
-                if b <= 5:
+                (m, side), *_ = [(m, pair.index(b)) for m, pair in enumerate(SENDS) if b in pair]
+                kept = jnp.where(core == side, 1.0, 0.0) * (0.5**12)
+                row = pl.ds(m, 1)
+                if side == 0:
                     keep_ref[h, row, :] = parts[h] * kept
                     give_ref[h, row, :] = parts[h] * (0.5**12 - kept)
                 else:
-                    keep_ref[h, row, :] += parts[h] * kept
-                    give_ref[h, row, :] += parts[h] * (0.5**12 - kept)
+                    late.append((h, row, parts[h] * kept, parts[h] * (0.5**12 - kept)))
+    if last:
+        for h, row, kept, given in late:
+            keep_ref[h, row, :] += kept
+            give_ref[h, row, :] += given
 
 
 def joined_sums(keep_ref, got_ref, *out_refs):
@@ -214,16 +224,13 @@
     other_ref[...] = jnp.where(first, total[1:], total[:1])
 
 
-STAGES = ((0, 1, 2, 3, 4), (5, 6, 7), (8, 9, 10))
-
-
 def all_sums(held, genes):
     half = genes // 2
     vmem = pl.BlockSpec(memory_space=pltpu.VMEM)
     done = []
     for number, new in enumerate(STAGES):
         first, last = number == 0, number == len(STAGES) - 1
-        pairs = [p for p in PAIRS if max(p[:2]) in new]
+        pairs = [p for p in PAIRS if p[1] in new]
         blocks = sorted({b for p in pairs for b in p[:2]})
         args = [h for b in blocks for h in held[b]] + done
         out_shape = [jax.ShapeDtypeStruct((2, 16, half), jnp.float32)]
@@ -264,6 +271,7 @@
 def on_device(expression):
     genes, _ = expression.shape
     other = fetch(expression, (0, 0, 0), 1)
+    (expression,) = small(bring, [expression], 4 * 2**20)(expression)
     held = [small(standardize, [expression] * 2, 8 * 2**20)(expression, other)]
     got = {DELTA[0]: held[0][0]}
     for b, (d, parent) in enumerate(OFFSETS):
@@ -274,8 +282,10 @@
         held.append((got[d], fetch(got[d], (0, 0, 0), 1)))
     own, keep, give = all_sums(held, genes)
     got = fetch(give, (0, 0, 0), 1)
-    joined = small(joined_sums, [own] * 5)(keep, got)
-    arrived = [deliver(v, DELTA[1 + m], DELTA[6 + m]) for m, v in enumerate(joined)]
+    joined = small(joined_sums, [own] * len(SENDS))(keep, got)
+    arrived = []
+    for m, (b0, b1) in enumerate(SENDS):
+        arrived.append(deliver(joined[m], DELTA[b0], DELTA[b1]))
     mine, other = small(owner_sums, [own[:1]] * 2)(own, *arrived)
     return (mine + fetch(other, (0, 0, 0), 1)).reshape(genes // 2) - 1.0
 

time: 80.5 us -> 79.4 us (0.986)
  waiting for transfers between devices: 30.2 us -> 24.1 us
  starting transfers between devices: 38.1 us -> 42.2 us
    ppermute x23, waiting for transfers between devices: 25.4 us -> 20.9 us  [fetch(): return lax.ppermute(value, ALL, pairs)]
    ppermute x23, starting transfers between devices: 29.3 us -> 33.6 us  [fetch(): return lax.ppermute(value, ALL, pairs)]
    ppermute x5, waiting for transfers between devices: 4.82 us -> 3.17 us  [deliver(): return lax.ppermute(value, ALL, pairs)]
    pallas_call x3 -> x5, Pallas kernels: 9.95 us -> 10.7 us  [all_sums(): done = list(call(*args))]
  transfers between devices with their start and end apart: 28 -> 28, of which waited for: 11 -> 12; matrix products, arithmetic and copies ran while one was open for 0% -> 0% of each run, Pallas kernels for 8% -> 12%
where the time goes in v2:
time: 79.4 us; the launch traced here: 79.1 us
  starting transfers between devices  42.2 us (53%)
  waiting for transfers between devices  24.1 us (30%)
  Pallas kernels  11.2 us (14%)
  local copies, waits for them, and re-layouts  1 us (1%)
    ppermute x23, starting transfers between devices, fetch(): return lax.ppermute(value, ALL, pairs)  33.6 us
    ppermute x23, waiting for transfers between devices, fetch(): return lax.ppermute(value, ALL, pairs)  20.9 us
    pallas_call x5, Pallas kernels, all_sums(): done = list(call(*args))  10.7 us
    ppermute x5, starting transfers between devices, deliver(): return lax.ppermute(value, ALL, pairs)  8.58 us
    ppermute x5, waiting for transfers between devices, deliver(): return lax.ppermute(value, ALL, pairs)  3.17 us
  transfers between devices with their start and end apart: 28, of which 12 were waited for; matrix products, arithmetic and copies ran while one was open for 0% of the time, Pallas kernels for 12%

profile of v2, /device:TPU:1, one launch (start us, length us, event | category | flops | bytes accessed | tf_op | source)
XLA Modules:
  0.0 79.1 jit_solution(6873062265545279123)
XLA Ops:
  0.0 1.4 %collective-permute-start = (bf16[384,512]{1,0:T(8,128)(2,1)}, bf16[384,512]{1,0:T(8,128)(2,1)S(1)}, u32[]{:S(2)}, u32[]{:S(2)}) collective-permute-start(bf16[384,512]{1,0:T(8,128)(2,1)} %in_ref.1), channel_id=1, source_target_pairs={{1,0},{0,1},{17,16},{16,17},{33,32},{32,33},{49,48},{48,49},{5,4},... | collective-permute-start | bytes 1179656 | tf_op jit(solution)/shard_map/ppermute | solution.py:74
  1.4 1.0 %copy-done = bf16[384,512]{1,0:T(8,128)(2,1)S(1)} copy-done((bf16[384,512]{1,0:T(8,128)(2,1)S(1)}, bf16[384,512]{1,0:T(8,128)(2,1)}, u32[]{:S(2)}) %copy-start) | copy-done | bytes 393240
  3.4 3.8 %collective-permute-start.6 = (bf16[384,512]{1,0:T(8,128)(2,1)S(1)}, bf16[384,512]{1,0:T(8,128)(2,1)S(1)}, u32[]{:S(2)}, u32[]{:S(2)}) collective-permute-start(bf16[384,512]{1,0:T(8,128)(2,1)S(1)} %get-tuple-element.17.refs_0_), channel_id=1, source_target_pairs={{70,0},{71,1},{86,16},{87,17},{102,32},{103,33},{118,48},{119,49},... | collective-permute-start | bytes 1179656 | tf_op jit(solution)/shard_map/ppermute | solution.py:74
  7.2 2.8 %collective-permute-start.9 = (bf16[384,512]{1,0:T(8,128)(2,1)S(1)}, bf16[384,512]{1,0:T(8,128)(2,1)S(1)}, u32[]{:S(2)}, u32[]{:S(2)}) collective-permute-start(bf16[384,512]{1,0:T(8,128)(2,1)S(1)} %get-tuple-element.17.refs_0_), channel_id=1, source_target_pairs={{50,0},{51,1},{2,16},{3,17},{18,32},{19,33},{34,48},{35,49},{54,4}... | collective-permute-start | bytes 1179656 | tf_op jit(solution)/shard_map/ppermute | solution.py:74
  10.0 1.0 %collective-permute-start.1 = (bf16[384,512]{1,0:T(8,128)(2,1)S(1)}, bf16[384,512]{1,0:T(8,128)(2,1)S(1)}, u32[]{:S(2)}, u32[]{:S(2)}) collective-permute-start(bf16[384,512]{1,0:T(8,128)(2,1)S(1)} %get-tuple-element.17.refs_0_), channel_id=1, source_target_pairs={{16,0},{17,1},{32,16},{33,17},{48,32},{49,33},{0,48},{1,49},{20,4}... | collective-permute-start | bytes 1179656 | tf_op jit(solution)/shard_map/ppermute | solution.py:74
  11.1 2.7 %collective-permute-start.12 = (bf16[384,512]{1,0:T(8,128)(2,1)S(1)}, bf16[384,512]{1,0:T(8,128)(2,1)S(1)}, u32[]{:S(2)}, u32[]{:S(2)}) collective-permute-start(bf16[384,512]{1,0:T(8,128)(2,1)S(1)} %get-tuple-element.17.refs_0_), channel_id=1, source_target_pairs={{4,0},{5,1},{20,16},{21,17},{36,32},{37,33},{52,48},{53,49},{8,4},... | collective-permute-start | bytes 1179656 | tf_op jit(solution)/shard_map/ppermute | solution.py:74
  13.8 2.2 %collective-permute-done.6.refs_4_ = bf16[384,512]{1,0:T(8,128)(2,1)S(1)} collective-permute-done((bf16[384,512]{1,0:T(8,128)(2,1)S(1)}, bf16[384,512]{1,0:T(8,128)(2,1)S(1)}, u32[]{:S(2)}, u32[]{:S(2)}) %collective-permute-start.6) | collective-permute-done | bytes 393248 | tf_op jit(solution)/shard_map/ppermute | solution.py:74
  15.9 1.3 %collective-permute-start.15 = (bf16[384,512]{1,0:T(8,128)(2,1)S(1)}, bf16[384,512]{1,0:T(8,128)(2,1)S(1)}, u32[]{:S(2)}, u32[]{:S(2)}) collective-permute-start(bf16[384,512]{1,0:T(8,128)(2,1)S(1)} %collective-permute-done.6.refs_4_), channel_id=1, source_target_pairs={{1,0},{0,1},{17,16},{16,17},{33,32},{32,33},{49,48},{48,49},{5,4},... | collective-permute-start | bytes 1179656 | tf_op jit(solution)/shard_map/ppermute | solution.py:74
  17.2 1.2 %collective-permute-done.3.refs_2_ = bf16[384,512]{1,0:T(8,128)(2,1)S(1)} collective-permute-done((bf16[384,512]{1,0:T(8,128)(2,1)S(1)}, bf16[384,512]{1,0:T(8,128)(2,1)S(1)}, u32[]{:S(2)}, u32[]{:S(2)}) %collective-permute-start.3) | collective-permute-done | bytes 393248 | tf_op jit(solution)/shard_map/ppermute | solution.py:74
  18.5 1.5 %collective-permute-start.14 = (bf16[384,512]{1,0:T(8,128)(2,1)S(1)}, bf16[384,512]{1,0:T(8,128)(2,1)S(1)}, u32[]{:S(2)}, u32[]{:S(2)}) collective-permute-start(bf16[384,512]{1,0:T(8,128)(2,1)S(1)} %collective-permute-done.3.refs_2_), channel_id=1, source_target_pairs={{1,0},{0,1},{17,16},{16,17},{33,32},{32,33},{49,48},{48,49},{5,4},... | collective-permute-start | bytes 1179656 | tf_op jit(solution)/shard_map/ppermute | solution.py:74
  20.8 1.2 %collective-permute-start.16 = (bf16[384,512]{1,0:T(8,128)(2,1)S(1)}, bf16[384,512]{1,0:T(8,128)(2,1)S(1)}, u32[]{:S(2)}, u32[]{:S(2)}) collective-permute-start(bf16[384,512]{1,0:T(8,128)(2,1)S(1)} %collective-permute-done.9.refs_6_), channel_id=1, source_target_pairs={{1,0},{0,1},{17,16},{16,17},{33,32},{32,33},{49,48},{48,49},{5,4},... | collective-permute-start | bytes 1179656 | tf_op jit(solution)/shard_map/ppermute | solution.py:74
  22.0 3.7 %collective-permute-done.12.refs_14_.refs_8_ = bf16[384,512]{1,0:T(8,128)(2,1)S(1)} collective-permute-done((bf16[384,512]{1,0:T(8,128)(2,1)S(1)}, bf16[384,512]{1,0:T(8,128)(2,1)S(1)}, u32[]{:S(2)}, u32[]{:S(2)}) %collective-permute-start.12) | collective-permute-done | bytes 393248 | tf_op jit(solution)/shard_map/ppermute | solution.py:74
  25.7 1.3 %collective-permute-start.10 = (bf16[384,512]{1,0:T(8,128)(2,1)S(1)}, bf16[384,512]{1,0:T(8,128)(2,1)S(1)}, u32[]{:S(2)}, u32[]{:S(2)}) collective-permute-start(bf16[384,512]{1,0:T(8,128)(2,1)S(1)} %collective-permute-done.9.refs_6_), channel_id=1, source_target_pairs={{2,0},{3,1},{18,16},{19,17},{34,32},{35,33},{50,48},{51,49},{6,4},... | collective-permute-start | bytes 1179656 | tf_op jit(solution)/shard_map/ppermute | solution.py:74
  27.9 3.6 %collective-permute-start.4 = (bf16[384,512]{1,0:T(8,128)(2,1)S(1)}, bf16[384,512]{1,0:T(8,128)(2,1)S(1)}, u32[]{:S(2)}, u32[]{:S(2)}) collective-permute-start(bf16[384,512]{1,0:T(8,128)(2,1)S(1)} %collective-permute-done.3.refs_2_), channel_id=1, source_target_pairs={{32,0},{33,1},{48,16},{49,17},{0,32},{1,33},{16,48},{17,49},{36,4}... | collective-permute-start | bytes 1179656 | tf_op jit(solution)/shard_map/ppermute | solution.py:74
  32.3 3.6 %collective-permute-done.10.refs_10_.refs_8_.refs_6_ = bf16[384,512]{1,0:T(8,128)(2,1)S(1)} collective-permute-done((bf16[384,512]{1,0:T(8,128)(2,1)S(1)}, bf16[384,512]{1,0:T(8,128)(2,1)S(1)}, u32[]{:S(2)}, u32[]{:S(2)}) %collective-permute-start.10) | collective-permute-done | bytes 393248 | tf_op jit(solution)/shard_map/ppermute | solution.py:74
  35.9 1.3 %collective-permute-start.11 = (bf16[384,512]{1,0:T(8,128)(2,1)S(1)}, bf16[384,512]{1,0:T(8,128)(2,1)S(1)}, u32[]{:S(2)}, u32[]{:S(2)}) collective-permute-start(bf16[384,512]{1,0:T(8,128)(2,1)S(1)} %collective-permute-done.10.refs_10_.refs_8_.refs_6_), channel_id=1, source_target_pairs={{1,0},{0,1},{17,16},{16,17},{33,32},{32,33},{49,48},{48,49},{5,4},... | collective-permute-start | bytes 1179656 | tf_op jit(solution)/shard_map/ppermute | solution.py:74
  38.1 1.6 %collective-permute-start.18 = (bf16[384,512]{1,0:T(8,128)(2,1)S(1)}, bf16[384,512]{1,0:T(8,128)(2,1)S(1)}, u32[]{:S(2)}, u32[]{:S(2)}) collective-permute-start(bf16[384,512]{1,0:T(8,128)(2,1)S(1)} %collective-permute-done.17.refs_10_), channel_id=1, source_target_pairs={{1,0},{0,1},{17,16},{16,17},{33,32},{32,33},{49,48},{48,49},{5,4},... | collective-permute-start | bytes 1179656 | tf_op jit(solution)/shard_map/ppermute | solution.py:74
  39.7 0.9 %collective-permute-start.20 = (bf16[384,512]{1,0:T(8,128)(2,1)S(1)}, bf16[384,512]{1,0:T(8,128)(2,1)S(1)}, u32[]{:S(2)}, u32[]{:S(2)}) collective-permute-start(bf16[384,512]{1,0:T(8,128)(2,1)S(1)} %collective-permute-done.19.refs_12_), channel_id=1, source_target_pairs={{1,0},{0,1},{17,16},{16,17},{33,32},{32,33},{49,48},{48,49},{5,4},... | collective-permute-start | bytes 1179656 | tf_op jit(solution)/shard_map/ppermute | solution.py:74
  40.6 2.5 %collective-permute-start.13 = (bf16[384,512]{1,0:T(8,128)(2,1)S(1)}, bf16[384,512]{1,0:T(8,128)(2,1)S(1)}, u32[]{:S(2)}, u32[]{:S(2)}) collective-permute-start(bf16[384,512]{1,0:T(8,128)(2,1)S(1)} %collective-permute-done.12.refs_14_.refs_8_), channel_id=1, source_target_pairs={{1,0},{0,1},{17,16},{16,17},{33,32},{32,33},{49,48},{48,49},{5,4},... | collective-permute-start | bytes 1179656 | tf_op jit(solution)/shard_map/ppermute | solution.py:74
  43.1 6.4 %collective-permute-done.7.refs_4_ = bf16[384,512]{1,0:T(8,128)(2,1)S(1)} collective-permute-done((bf16[384,512]{1,0:T(8,128)(2,1)S(1)}, bf16[384,512]{1,0:T(8,128)(2,1)S(1)}, u32[]{:S(2)}, u32[]{:S(2)}) %collective-permute-start.7) | collective-permute-done | bytes 393248 | tf_op jit(solution)/shard_map/ppermute | solution.py:74
  50.0 3.1 %shard_map.19.refs_12_ = f32[2,16,192]{2,1,0:T(8,128)S(1)} custom-call(bf16[384,512]{1,0:T(8,128)(2,1)S(1)} %get-tuple-element.17.refs_0_, bf16[384,512]{1,0:T(8,128)(2,1)S(1)} %get-tuple-element.18.refs_1_, bf16[384,512]{1,0:T(8,128)(2,1)S(1)} %collective-permute-done.3.refs_2_, bf16[384,512]{1,0:T(8,128)(2,1)S(1)} %collective-permute-done.14.refs_3_, ...), custom_call_target="tpu_custom_call" | custom-call | flops 1660944384 | bytes 1048576 | tf_op jit(solution)/shard_map/pallas_call | solution.py:257
  53.1 1.5 %shard_map.20.refs_14_ = f32[2,16,192]{2,1,0:T(8,128)S(1)} custom-call(bf16[384,512]{1,0:T(8,128)(2,1)S(1)} %get-tuple-element.17.refs_0_, bf16[384,512]{1,0:T(8,128)(2,1)S(1)} %get-tuple-element.18.refs_1_, bf16[384,512]{1,0:T(8,128)(2,1)S(1)} %collective-permute-done.3.refs_2_, bf16[384,512]{1,0:T(8,128)(2,1)S(1)} %collective-permute-done.14.refs_3_, ...), custom_call_target="tpu_custom_call" | custom-call | flops 754974720 | bytes 1048576 | tf_op jit(solution)/shard_map/pallas_call | solution.py:257
  54.6 1.9 %shard_map.21.refs_16_ = f32[2,16,192]{2,1,0:T(8,128)S(1)} custom-call(bf16[384,512]{1,0:T(8,128)(2,1)S(1)} %get-tuple-element.17.refs_0_, bf16[384,512]{1,0:T(8,128)(2,1)S(1)} %get-tuple-element.18.refs_1_, bf16[384,512]{1,0:T(8,128)(2,1)S(1)} %collective-permute-done.3.refs_2_, bf16[384,512]{1,0:T(8,128)(2,1)S(1)} %collective-permute-done.14.refs_3_, ...), custom_call_target="tpu_custom_call" | custom-call | flops 1056964608 | bytes 1048576 | tf_op jit(solution)/shard_map/pallas_call | solution.py:257
  56.5 2.7 %shard_map.22.refs_10_ = f32[2,16,192]{2,1,0:T(8,128)S(1)} custom-call(bf16[384,512]{1,0:T(8,128)(2,1)S(1)} %get-tuple-element.17.refs_0_, bf16[384,512]{1,0:T(8,128)(2,1)S(1)} %get-tuple-element.18.refs_1_, bf16[384,512]{1,0:T(8,128)(2,1)S(1)} %collective-permute-done.3.refs_2_, bf16[384,512]{1,0:T(8,128)(2,1)S(1)} %collective-permute-done.14.refs_3_, ...), custom_call_target="tpu_custom_call" | custom-call | flops 1358954496 | bytes 1048576 | tf_op jit(solution)/shard_map/pallas_call | solution.py:257
  59.2 1.6 %shard_map.23 = (f32[2,192]{1,0:T(2,128)S(1)}, f32[2,8,192]{2,1,0:T(8,128)S(1)}, f32[2,8,192]{2,1,0:T(8,128)S(1)}) custom-call(bf16[384,512]{1,0:T(8,128)(2,1)S(1)} %collective-permute-done.1.refs_8_.refs_0_, bf16[384,512]{1,0:T(8,128)(2,1)S(1)} %collective-permute-done.2.refs_9_.refs_1_, bf16[384,512]{1,0:T(8,128)(2,1)S(1)} %collective-permute-done.4.refs_8_.refs_2_, ...), custom_call_target="tpu_custom_call" | custom-call | flops 603979776 | bytes 1048576 | tf_op jit(solution)/shard_map/pallas_call | solution.py:257
  62.2 1.6 %collective-permute-start.22 = (f32[2,192]{1,0:T(2,128)S(1)}, f32[2,192]{1,0:T(2,128)S(1)}, u32[]{:S(2)}, u32[]{:S(2)}) collective-permute-start(f32[2,192]{1,0:T(2,128)S(1)} %get-tuple-element.22), channel_id=1, source_target_pairs={{0,118},{1,113},{16,70},{17,65},{32,86},{33,81},{48,102},{49,97},{... | collective-permute-start | bytes 4616 | tf_op jit(solution)/shard_map/ppermute | solution.py:83
  63.8 2.5 %collective-permute-start.23 = (f32[2,192]{1,0:T(2,128)S(1)}, f32[2,192]{1,0:T(2,128)S(1)}, u32[]{:S(2)}, u32[]{:S(2)}) collective-permute-start(f32[2,192]{1,0:T(2,128)S(1)} %get-tuple-element.23), channel_id=1, source_target_pairs={{0,44},{1,69},{16,60},{17,85},{32,12},{33,101},{48,28},{49,117},{4... | collective-permute-start | bytes 4616 | tf_op jit(solution)/shard_map/ppermute | solution.py:83
  66.3 2.3 %collective-permute-start.24 = (f32[2,192]{1,0:T(2,128)S(1)}, f32[2,192]{1,0:T(2,128)S(1)}, u32[]{:S(2)}, u32[]{:S(2)}) collective-permute-start(f32[2,192]{1,0:T(2,128)S(1)} %get-tuple-element.24), channel_id=1, source_target_pairs={{0,70},{1,51},{16,86},{17,3},{32,102},{33,19},{48,118},{49,35},{4,... | collective-permute-start | bytes 4616 | tf_op jit(solution)/shard_map/ppermute | solution.py:83
  68.5 1.7 %collective-permute-start.25 = (f32[2,192]{1,0:T(2,128)S(1)}, f32[2,192]{1,0:T(2,128)S(1)}, u32[]{:S(2)}, u32[]{:S(2)}) collective-permute-start(f32[2,192]{1,0:T(2,128)S(1)} %get-tuple-element.25), channel_id=1, source_target_pairs={{0,28},{1,13},{16,44},{17,29},{32,60},{33,45},{48,12},{49,61},{4,1... | collective-permute-start | bytes 4616 | tf_op jit(solution)/shard_map/ppermute | solution.py:83
  70.8 1.2 %collective-permute-done.25.refs_3_ = f32[2,192]{1,0:T(2,128)S(1)} collective-permute-done((f32[2,192]{1,0:T(2,128)S(1)}, f32[2,192]{1,0:T(2,128)S(1)}, u32[]{:S(2)}, u32[]{:S(2)}) %collective-permute-start.25) | collective-permute-done | bytes 1568 | tf_op jit(solution)/shard_map/ppermute | solution.py:83
  72.0 1.9 %collective-permute-done.26.refs_4_ = f32[2,192]{1,0:T(2,128)S(1)} collective-permute-done((f32[2,192]{1,0:T(2,128)S(1)}, f32[2,192]{1,0:T(2,128)S(1)}, u32[]{:S(2)}, u32[]{:S(2)}) %collective-permute-start.26) | collective-permute-done | bytes 1568 | tf_op jit(solution)/shard_map/ppermute | solution.py:83
  73.9 3.8 %collective-permute-start.27 = (f32[1,192]{1,0:T(1,128)S(1)}, f32[1,192]{1,0:T(1,128)S(1)}, u32[]{:S(2)}, u32[]{:S(2)}) collective-permute-start(f32[1,192]{1,0:T(1,128)S(1)} %get-tuple-element.28), channel_id=1, source_target_pairs={{1,0},{0,1},{17,16},{16,17},{33,32},{32,33},{49,48},{48,49},{5,4},... | collective-permute-start | bytes 2312 | tf_op jit(solution)/shard_map/ppermute | solution.py:74
  (36 shorter events, 8.2 us)
Async XLA Ops:
  0.0 2.9 %collective-permute-start = (bf16[384,512]{1,0:T(8,128)(2,1)}, bf16[384,512]{1,0:T(8,128)(2,1)S(1)}, u32[]{:S(2)}, u32[]{:S(2)}) collective-permute-start(bf16[384,512]{1,0:T(8,128)(2,1)} %in_ref.1), channel_id=1, source_target_pairs={{1,0},{0,1},{17,16},{16,17},{33,32},{32,33},{49,48},{48,49},{5,4},... | collective-permute-start | bytes 1179656 | tf_op jit(solution)/shard_map/ppermute | solution.py:74
  1.4 1.0 %copy-start = (bf16[384,512]{1,0:T(8,128)(2,1)S(1)}, bf16[384,512]{1,0:T(8,128)(2,1)}, u32[]{:S(2)}) copy-start(bf16[384,512]{1,0:T(8,128)(2,1)} %in_ref.1) | copy-start | bytes 1179652
  3.4 12.5 %collective-permute-start.6 = (bf16[384,512]{1,0:T(8,128)(2,1)S(1)}, bf16[384,512]{1,0:T(8,128)(2,1)S(1)}, u32[]{:S(2)}, u32[]{:S(2)}) collective-permute-start(bf16[384,512]{1,0:T(8,128)(2,1)S(1)} %get-tuple-element.17.refs_0_), channel_id=1, source_target_pairs={{70,0},{71,1},{86,16},{87,17},{102,32},{103,33},{118,48},{119,49},... | collective-permute-start | bytes 1179656 | tf_op jit(solution)/shard_map/ppermute | solution.py:74
  7.2 11.2 %collective-permute-start.3 = (bf16[384,512]{1,0:T(8,128)(2,1)S(1)}, bf16[384,512]{1,0:T(8,128)(2,1)S(1)}, u32[]{:S(2)}, u32[]{:S(2)}) collective-permute-start(bf16[384,512]{1,0:T(8,128)(2,1)S(1)} %get-tuple-element.17.refs_0_), channel_id=1, source_target_pairs={{12,0},{13,1},{28,16},{29,17},{44,32},{45,33},{60,48},{61,49},{0,4... | collective-permute-start | bytes 1179656 | tf_op jit(solution)/shard_map/ppermute | solution.py:74
  7.2 13.5 %collective-permute-start.9 = (bf16[384,512]{1,0:T(8,128)(2,1)S(1)}, bf16[384,512]{1,0:T(8,128)(2,1)S(1)}, u32[]{:S(2)}, u32[]{:S(2)}) collective-permute-start(bf16[384,512]{1,0:T(8,128)(2,1)S(1)} %get-tuple-element.17.refs_0_), channel_id=1, source_target_pairs={{50,0},{51,1},{2,16},{3,17},{18,32},{19,33},{34,48},{35,49},{54,4}... | collective-permute-start | bytes 1179656 | tf_op jit(solution)/shard_map/ppermute | solution.py:74
  10.0 11.9 %collective-permute-start.1 = (bf16[384,512]{1,0:T(8,128)(2,1)S(1)}, bf16[384,512]{1,0:T(8,128)(2,1)S(1)}, u32[]{:S(2)}, u32[]{:S(2)}) collective-permute-start(bf16[384,512]{1,0:T(8,128)(2,1)S(1)} %get-tuple-element.17.refs_0_), channel_id=1, source_target_pairs={{16,0},{17,1},{32,16},{33,17},{48,32},{49,33},{0,48},{1,49},{20,4}... | collective-permute-start | bytes 1179656 | tf_op jit(solution)/shard_map/ppermute | solution.py:74
  11.1 14.6 %collective-permute-start.12 = (bf16[384,512]{1,0:T(8,128)(2,1)S(1)}, bf16[384,512]{1,0:T(8,128)(2,1)S(1)}, u32[]{:S(2)}, u32[]{:S(2)}) collective-permute-start(bf16[384,512]{1,0:T(8,128)(2,1)S(1)} %get-tuple-element.17.refs_0_), channel_id=1, source_target_pairs={{4,0},{5,1},{20,16},{21,17},{36,32},{37,33},{52,48},{53,49},{8,4},... | collective-permute-start | bytes 1179656 | tf_op jit(solution)/shard_map/ppermute | solution.py:74
  15.9 11.0 %collective-permute-start.15 = (bf16[384,512]{1,0:T(8,128)(2,1)S(1)}, bf16[384,512]{1,0:T(8,128)(2,1)S(1)}, u32[]{:S(2)}, u32[]{:S(2)}) collective-permute-start(bf16[384,512]{1,0:T(8,128)(2,1)S(1)} %collective-permute-done.6.refs_4_), channel_id=1, source_target_pairs={{1,0},{0,1},{17,16},{16,17},{33,32},{32,33},{49,48},{48,49},{5,4},... | collective-permute-start | bytes 1179656 | tf_op jit(solution)/shard_map/ppermute | solution.py:74
  18.5 8.7 %collective-permute-start.14 = (bf16[384,512]{1,0:T(8,128)(2,1)S(1)}, bf16[384,512]{1,0:T(8,128)(2,1)S(1)}, u32[]{:S(2)}, u32[]{:S(2)}) collective-permute-start(bf16[384,512]{1,0:T(8,128)(2,1)S(1)} %collective-permute-done.3.refs_2_), channel_id=1, source_target_pairs={{1,0},{0,1},{17,16},{16,17},{33,32},{32,33},{49,48},{48,49},{5,4},... | collective-permute-start | bytes 1179656 | tf_op jit(solution)/shard_map/ppermute | solution.py:74
  20.8 7.2 %collective-permute-start.16 = (bf16[384,512]{1,0:T(8,128)(2,1)S(1)}, bf16[384,512]{1,0:T(8,128)(2,1)S(1)}, u32[]{:S(2)}, u32[]{:S(2)}) collective-permute-start(bf16[384,512]{1,0:T(8,128)(2,1)S(1)} %collective-permute-done.9.refs_6_), channel_id=1, source_target_pairs={{1,0},{0,1},{17,16},{16,17},{33,32},{32,33},{49,48},{48,49},{5,4},... | collective-permute-start | bytes 1179656 | tf_op jit(solution)/shard_map/ppermute | solution.py:74
  22.0 9.5 %collective-permute-start.2 = (bf16[384,512]{1,0:T(8,128)(2,1)S(1)}, bf16[384,512]{1,0:T(8,128)(2,1)S(1)}, u32[]{:S(2)}, u32[]{:S(2)}) collective-permute-start(bf16[384,512]{1,0:T(8,128)(2,1)S(1)} %collective-permute-done.1.refs_8_.refs_0_), channel_id=1, source_target_pairs={{1,0},{0,1},{17,16},{16,17},{33,32},{32,33},{49,48},{48,49},{5,4},... | collective-permute-start | bytes 1179656 | tf_op jit(solution)/shard_map/ppermute | solution.py:74
  25.7 10.2 %collective-permute-start.10 = (bf16[384,512]{1,0:T(8,128)(2,1)S(1)}, bf16[384,512]{1,0:T(8,128)(2,1)S(1)}, u32[]{:S(2)}, u32[]{:S(2)}) collective-permute-start(bf16[384,512]{1,0:T(8,128)(2,1)S(1)} %collective-permute-done.9.refs_6_), channel_id=1, source_target_pairs={{2,0},{3,1},{18,16},{19,17},{34,32},{35,33},{50,48},{51,49},{6,4},... | collective-permute-start | bytes 1179656 | tf_op jit(solution)/shard_map/ppermute | solution.py:74
  26.9 11.1 %collective-permute-start.17 = (bf16[384,512]{1,0:T(8,128)(2,1)S(1)}, bf16[384,512]{1,0:T(8,128)(2,1)S(1)}, u32[]{:S(2)}, u32[]{:S(2)}) collective-permute-start(bf16[384,512]{1,0:T(8,128)(2,1)S(1)} %collective-permute-done.6.refs_4_), channel_id=1, source_target_pairs={{66,0},{67,1},{82,16},{83,17},{98,32},{99,33},{114,48},{115,49},{7... | collective-permute-start | bytes 1179656 | tf_op jit(solution)/shard_map/ppermute | solution.py:74
  27.1 12.5 %collective-permute-start.19 = (bf16[384,512]{1,0:T(8,128)(2,1)S(1)}, bf16[384,512]{1,0:T(8,128)(2,1)S(1)}, u32[]{:S(2)}, u32[]{:S(2)}) collective-permute-start(bf16[384,512]{1,0:T(8,128)(2,1)S(1)} %collective-permute-done.1.refs_8_.refs_0_), channel_id=1, source_target_pairs={{12,0},{13,1},{28,16},{29,17},{44,32},{45,33},{60,48},{61,49},{0,4... | collective-permute-start | bytes 1179656 | tf_op jit(solution)/shard_map/ppermute | solution.py:74
  27.9 12.7 %collective-permute-start.4 = (bf16[384,512]{1,0:T(8,128)(2,1)S(1)}, bf16[384,512]{1,0:T(8,128)(2,1)S(1)}, u32[]{:S(2)}, u32[]{:S(2)}) collective-permute-start(bf16[384,512]{1,0:T(8,128)(2,1)S(1)} %collective-permute-done.3.refs_2_), channel_id=1, source_target_pairs={{32,0},{33,1},{48,16},{49,17},{0,32},{1,33},{16,48},{17,49},{36,4}... | collective-permute-start | bytes 1179656 | tf_op jit(solution)/shard_map/ppermute | solution.py:74
  31.5 18.0 %collective-permute-start.7 = (bf16[384,512]{1,0:T(8,128)(2,1)S(1)}, bf16[384,512]{1,0:T(8,128)(2,1)S(1)}, u32[]{:S(2)}, u32[]{:S(2)}) collective-permute-start(bf16[384,512]{1,0:T(8,128)(2,1)S(1)} %collective-permute-done.6.refs_4_), channel_id=1, source_target_pairs={{48,0},{49,1},{0,16},{1,17},{16,32},{17,33},{32,48},{33,49},{52,4}... | collective-permute-start | bytes 1179656 | tf_op jit(solution)/shard_map/ppermute | solution.py:74
  35.9 14.2 %collective-permute-start.11 = (bf16[384,512]{1,0:T(8,128)(2,1)S(1)}, bf16[384,512]{1,0:T(8,128)(2,1)S(1)}, u32[]{:S(2)}, u32[]{:S(2)}) collective-permute-start(bf16[384,512]{1,0:T(8,128)(2,1)S(1)} %collective-permute-done.10.refs_10_.refs_8_.refs_6_), channel_id=1, source_target_pairs={{1,0},{0,1},{17,16},{16,17},{33,32},{32,33},{49,48},{48,49},{5,4},... | collective-permute-start | bytes 1179656 | tf_op jit(solution)/shard_map/ppermute | solution.py:74
  38.1 16.5 %collective-permute-start.18 = (bf16[384,512]{1,0:T(8,128)(2,1)S(1)}, bf16[384,512]{1,0:T(8,128)(2,1)S(1)}, u32[]{:S(2)}, u32[]{:S(2)}) collective-permute-start(bf16[384,512]{1,0:T(8,128)(2,1)S(1)} %collective-permute-done.17.refs_10_), channel_id=1, source_target_pairs={{1,0},{0,1},{17,16},{16,17},{33,32},{32,33},{49,48},{48,49},{5,4},... | collective-permute-start | bytes 1179656 | tf_op jit(solution)/shard_map/ppermute | solution.py:74
  39.7 14.9 %collective-permute-start.20 = (bf16[384,512]{1,0:T(8,128)(2,1)S(1)}, bf16[384,512]{1,0:T(8,128)(2,1)S(1)}, u32[]{:S(2)}, u32[]{:S(2)}) collective-permute-start(bf16[384,512]{1,0:T(8,128)(2,1)S(1)} %collective-permute-done.19.refs_12_), channel_id=1, source_target_pairs={{1,0},{0,1},{17,16},{16,17},{33,32},{32,33},{49,48},{48,49},{5,4},... | collective-permute-start | bytes 1179656 | tf_op jit(solution)/shard_map/ppermute | solution.py:74
  40.6 15.9 %collective-permute-start.13 = (bf16[384,512]{1,0:T(8,128)(2,1)S(1)}, bf16[384,512]{1,0:T(8,128)(2,1)S(1)}, u32[]{:S(2)}, u32[]{:S(2)}) collective-permute-start(bf16[384,512]{1,0:T(8,128)(2,1)S(1)} %collective-permute-done.12.refs_14_.refs_8_), channel_id=1, source_target_pairs={{1,0},{0,1},{17,16},{16,17},{33,32},{32,33},{49,48},{48,49},{5,4},... | collective-permute-start | bytes 1179656 | tf_op jit(solution)/shard_map/ppermute | solution.py:74
  49.5 7.0 %collective-permute-start.5 = (bf16[384,512]{1,0:T(8,128)(2,1)S(1)}, bf16[384,512]{1,0:T(8,128)(2,1)S(1)}, u32[]{:S(2)}, u32[]{:S(2)}) collective-permute-start(bf16[384,512]{1,0:T(8,128)(2,1)S(1)} %collective-permute-done.4.refs_8_.refs_2_), channel_id=1, source_target_pairs={{1,0},{0,1},{17,16},{16,17},{33,32},{32,33},{49,48},{48,49},{5,4},... | collective-permute-start | bytes 1179656 | tf_op jit(solution)/shard_map/ppermute | solution.py:74
  50.0 9.2 %collective-permute-start.8 = (bf16[384,512]{1,0:T(8,128)(2,1)S(1)}, bf16[384,512]{1,0:T(8,128)(2,1)S(1)}, u32[]{:S(2)}, u32[]{:S(2)}) collective-permute-start(bf16[384,512]{1,0:T(8,128)(2,1)S(1)} %collective-permute-done.7.refs_4_), channel_id=1, source_target_pairs={{1,0},{0,1},{17,16},{16,17},{33,32},{32,33},{49,48},{48,49},{5,4},... | collective-permute-start | bytes 1179656 | tf_op jit(solution)/shard_map/ppermute | solution.py:74
  60.8 1.4 %collective-permute-start.21 = (f32[2,8,192]{2,1,0:T(8,128)S(1)}, f32[2,8,192]{2,1,0:T(8,128)S(1)}, u32[]{:S(2)}, u32[]{:S(2)}) collective-permute-start(f32[2,8,192]{2,1,0:T(8,128)S(1)} %get-tuple-element.21), channel_id=1, source_target_pairs={{1,0},{0,1},{17,16},{16,17},{33,32},{32,33},{49,48},{48,49},{5,4},... | collective-permute-start | bytes 36872 | tf_op jit(solution)/shard_map/ppermute | solution.py:74
  62.2 8.6 %collective-permute-start.22 = (f32[2,192]{1,0:T(2,128)S(1)}, f32[2,192]{1,0:T(2,128)S(1)}, u32[]{:S(2)}, u32[]{:S(2)}) collective-permute-start(f32[2,192]{1,0:T(2,128)S(1)} %get-tuple-element.22), channel_id=1, source_target_pairs={{0,118},{1,113},{16,70},{17,65},{32,86},{33,81},{48,102},{49,97},{... | collective-permute-start | bytes 4616 | tf_op jit(solution)/shard_map/ppermute | solution.py:83
  63.8 7.0 %collective-permute-start.23 = (f32[2,192]{1,0:T(2,128)S(1)}, f32[2,192]{1,0:T(2,128)S(1)}, u32[]{:S(2)}, u32[]{:S(2)}) collective-permute-start(f32[2,192]{1,0:T(2,128)S(1)} %get-tuple-element.23), channel_id=1, source_target_pairs={{0,44},{1,69},{16,60},{17,85},{32,12},{33,101},{48,28},{49,117},{4... | collective-permute-start | bytes 4616 | tf_op jit(solution)/shard_map/ppermute | solution.py:83
  66.3 4.5 %collective-permute-start.24 = (f32[2,192]{1,0:T(2,128)S(1)}, f32[2,192]{1,0:T(2,128)S(1)}, u32[]{:S(2)}, u32[]{:S(2)}) collective-permute-start(f32[2,192]{1,0:T(2,128)S(1)} %get-tuple-element.24), channel_id=1, source_target_pairs={{0,70},{1,51},{16,86},{17,3},{32,102},{33,19},{48,118},{49,35},{4,... | collective-permute-start | bytes 4616 | tf_op jit(solution)/shard_map/ppermute | solution.py:83
  68.5 3.5 %collective-permute-start.25 = (f32[2,192]{1,0:T(2,128)S(1)}, f32[2,192]{1,0:T(2,128)S(1)}, u32[]{:S(2)}, u32[]{:S(2)}) collective-permute-start(f32[2,192]{1,0:T(2,128)S(1)} %get-tuple-element.25), channel_id=1, source_target_pairs={{0,28},{1,13},{16,44},{17,29},{32,60},{33,45},{48,12},{49,61},{4,1... | collective-permute-start | bytes 4616 | tf_op jit(solution)/shard_map/ppermute | solution.py:83
  70.3 3.6 %collective-permute-start.26 = (f32[2,192]{1,0:T(2,128)S(1)}, f32[2,192]{1,0:T(2,128)S(1)}, u32[]{:S(2)}, u32[]{:S(2)}) collective-permute-start(f32[2,192]{1,0:T(2,128)S(1)} %get-tuple-element.26), channel_id=1, source_target_pairs={{0,16},{1,5},{16,32},{17,21},{32,48},{33,37},{48,0},{49,53},{4,20}... | collective-permute-start | bytes 4616 | tf_op jit(solution)/shard_map/ppermute | solution.py:83
  73.9 4.6 %collective-permute-start.27 = (f32[1,192]{1,0:T(1,128)S(1)}, f32[1,192]{1,0:T(1,128)S(1)}, u32[]{:S(2)}, u32[]{:S(2)}) collective-permute-start(f32[1,192]{1,0:T(1,128)S(1)} %get-tuple-element.28), channel_id=1, source_target_pairs={{1,0},{0,1},{17,16},{16,17},{33,32},{32,33},{49,48},{48,49},{5,4},... | collective-permute-start | bytes 2312 | tf_op jit(solution)/shard_map/ppermute | solution.py:74

commit v3 on v2

--- a/solution.py
+++ b/solution.py
@@ -20,19 +20,19 @@
 
 OFFSETS = (
     ((0, 0, 0), None),
-    ((0, 3, 0), None),
-    ((3, 1, 0), None),
-    ((1, 0, 3), None),
-    ((0, 0, 1), None),
-    ((0, 3, 2), (0, 3, 0)),
-    ((3, 1, 3), (3, 1, 0)),
-    ((2, 0, 3), (1, 0, 3)),
-    ((2, 1, 0), (3, 1, 0)),
-    ((0, 3, 1), (0, 0, 1)),
+    ((3, 3, 3), None),
+    ((1, 0, 0), None),
     ((0, 1, 0), None),
+    ((3, 0, 1), None),
+    ((1, 0, 1), (1, 0, 0)),
+    ((1, 0, 3), (1, 0, 0)),
+    ((0, 2, 0), (0, 1, 0)),
+    ((0, 3, 3), (3, 3, 3)),
+    ((3, 2, 3), (3, 3, 3)),
+    ((2, 0, 1), (3, 0, 1)),
 )
-STAGES = ((0, 1, 2, 3, 4), (7,), (8, 9), (10, 5), (6,))
-SENDS = ((6, 7), (5, 8), (2, 3), (9, 1), (4, 10))
+STAGES = ((0, 1, 2, 3, 4), (5,), (6, 7), (8, 9), (10,))
+SENDS = ((9, 10), (1, 8), (7, 4), (5, 6), (2, 3))
 DELTA = tuple(d for d, _ in OFFSETS)
 BLOCKS = len(DELTA)
 

time: 79.4 us -> 82.2 us (1.035)
  waiting for transfers between devices: 24.1 us -> 35.1 us
  starting transfers between devices: 42.2 us -> 34.2 us
    ppermute x23, waiting for transfers between devices: 20.9 us -> 32.7 us  [fetch(): return lax.ppermute(value, ALL, pairs)]
    ppermute x23, starting transfers between devices: 33.6 us -> 27.9 us  [fetch(): return lax.ppermute(value, ALL, pairs)]
    ppermute x5, starting transfers between devices: 8.58 us -> 6.3 us  [deliver(): return lax.ppermute(value, ALL, pairs)]
where the time goes in v3:
time: 82.2 us; the launch traced here: 82 us
  waiting for transfers between devices  35.1 us (43%)
  starting transfers between devices  34.2 us (42%)
  Pallas kernels  11.2 us (14%)
  local copies, waits for them, and re-layouts  1 us (1%)
    ppermute x23, waiting for transfers between devices, fetch(): return lax.ppermute(value, ALL, pairs)  32.7 us
    ppermute x23, starting transfers between devices, fetch(): return lax.ppermute(value, ALL, pairs)  27.9 us
    pallas_call x5, Pallas kernels, all_sums(): done = list(call(*args))  10.7 us
    ppermute x5, starting transfers between devices, deliver(): return lax.ppermute(value, ALL, pairs)  6.3 us
    ppermute x5, waiting for transfers between devices, deliver(): return lax.ppermute(value, ALL, pairs)  2.34 us
  transfers between devices with their start and end apart: 28, of which 12 were waited for; matrix products, arithmetic and copies ran while one was open for 0% of the time, Pallas kernels for 12%

profile of v3, /device:TPU:1, one launch (start us, length us, event | category | flops | bytes accessed | tf_op | source)
XLA Modules:
  0.0 82.0 jit_solution(3466628596375932557)
XLA Ops:
  0.0 1.4 %collective-permute-start = (bf16[384,512]{1,0:T(8,128)(2,1)}, bf16[384,512]{1,0:T(8,128)(2,1)S(1)}, u32[]{:S(2)}, u32[]{:S(2)}) collective-permute-start(bf16[384,512]{1,0:T(8,128)(2,1)} %in_ref.1), channel_id=1, source_target_pairs={{1,0},{0,1},{17,16},{16,17},{33,32},{32,33},{49,48},{48,49},{5,4},... | collective-permute-start | bytes 1179656 | tf_op jit(solution)/shard_map/ppermute | solution.py:74
  1.4 1.0 %copy-done = bf16[384,512]{1,0:T(8,128)(2,1)S(1)} copy-done((bf16[384,512]{1,0:T(8,128)(2,1)S(1)}, bf16[384,512]{1,0:T(8,128)(2,1)}, u32[]{:S(2)}) %copy-start) | copy-done | bytes 393240
  3.4 2.9 %collective-permute-start.1 = (bf16[384,512]{1,0:T(8,128)(2,1)S(1)}, bf16[384,512]{1,0:T(8,128)(2,1)S(1)}, u32[]{:S(2)}, u32[]{:S(2)}) collective-permute-start(bf16[384,512]{1,0:T(8,128)(2,1)S(1)} %get-tuple-element.17.refs_0_), channel_id=1, source_target_pairs={{4,0},{5,1},{20,16},{21,17},{36,32},{37,33},{52,48},{53,49},{8,4},... | collective-permute-start | bytes 1179656 | tf_op jit(solution)/shard_map/ppermute | solution.py:74
  6.3 2.5 %collective-permute-start.3 = (bf16[384,512]{1,0:T(8,128)(2,1)S(1)}, bf16[384,512]{1,0:T(8,128)(2,1)S(1)}, u32[]{:S(2)}, u32[]{:S(2)}) collective-permute-start(bf16[384,512]{1,0:T(8,128)(2,1)S(1)} %get-tuple-element.17.refs_0_), channel_id=1, source_target_pairs={{2,0},{3,1},{18,16},{19,17},{34,32},{35,33},{50,48},{51,49},{6,4},... | collective-permute-start | bytes 1179656 | tf_op jit(solution)/shard_map/ppermute | solution.py:74
  8.8 2.5 %collective-permute-start.9 = (bf16[384,512]{1,0:T(8,128)(2,1)S(1)}, bf16[384,512]{1,0:T(8,128)(2,1)S(1)}, u32[]{:S(2)}, u32[]{:S(2)}) collective-permute-start(bf16[384,512]{1,0:T(8,128)(2,1)S(1)} %get-tuple-element.17.refs_0_), channel_id=1, source_target_pairs={{82,0},{83,1},{98,16},{99,17},{114,32},{115,33},{66,48},{67,49},{8... | collective-permute-start | bytes 1179656 | tf_op jit(solution)/shard_map/ppermute | solution.py:74
  11.2 3.2 %collective-permute-done.1.refs_6_.refs_4_.refs_0_ = bf16[384,512]{1,0:T(8,128)(2,1)S(1)} collective-permute-done((bf16[384,512]{1,0:T(8,128)(2,1)S(1)}, bf16[384,512]{1,0:T(8,128)(2,1)S(1)}, u32[]{:S(2)}, u32[]{:S(2)}) %collective-permute-start.1) | collective-permute-done | bytes 393248 | tf_op jit(solution)/shard_map/ppermute | solution.py:74
  14.4 1.2 %collective-permute-start.2 = (bf16[384,512]{1,0:T(8,128)(2,1)S(1)}, bf16[384,512]{1,0:T(8,128)(2,1)S(1)}, u32[]{:S(2)}, u32[]{:S(2)}) collective-permute-start(bf16[384,512]{1,0:T(8,128)(2,1)S(1)} %collective-permute-done.1.refs_6_.refs_4_.refs_0_), channel_id=1, source_target_pairs={{1,0},{0,1},{17,16},{16,17},{33,32},{32,33},{49,48},{48,49},{5,4},... | collective-permute-start | bytes 1179656 | tf_op jit(solution)/shard_map/ppermute | solution.py:74
  15.6 1.0 %collective-permute-done.3.refs_4_.refs_2_ = bf16[384,512]{1,0:T(8,128)(2,1)S(1)} collective-permute-done((bf16[384,512]{1,0:T(8,128)(2,1)S(1)}, bf16[384,512]{1,0:T(8,128)(2,1)S(1)}, u32[]{:S(2)}, u32[]{:S(2)}) %collective-permute-start.3) | collective-permute-done | bytes 393248 | tf_op jit(solution)/shard_map/ppermute | solution.py:74
  16.6 1.5 %collective-permute-start.12 = (bf16[384,512]{1,0:T(8,128)(2,1)S(1)}, bf16[384,512]{1,0:T(8,128)(2,1)S(1)}, u32[]{:S(2)}, u32[]{:S(2)}) collective-permute-start(bf16[384,512]{1,0:T(8,128)(2,1)S(1)} %collective-permute-done.3.refs_4_.refs_2_), channel_id=1, source_target_pairs={{1,0},{0,1},{17,16},{16,17},{33,32},{32,33},{49,48},{48,49},{5,4},... | collective-permute-start | bytes 1179656 | tf_op jit(solution)/shard_map/ppermute | solution.py:74
  18.1 2.5 %collective-permute-done.9.refs_8_.refs_6_ = bf16[384,512]{1,0:T(8,128)(2,1)S(1)} collective-permute-done((bf16[384,512]{1,0:T(8,128)(2,1)S(1)}, bf16[384,512]{1,0:T(8,128)(2,1)S(1)}, u32[]{:S(2)}, u32[]{:S(2)}) %collective-permute-start.9) | collective-permute-done | bytes 393248 | tf_op jit(solution)/shard_map/ppermute | solution.py:74
  20.6 3.2 %collective-permute-start.13 = (bf16[384,512]{1,0:T(8,128)(2,1)S(1)}, bf16[384,512]{1,0:T(8,128)(2,1)S(1)}, u32[]{:S(2)}, u32[]{:S(2)}) collective-permute-start(bf16[384,512]{1,0:T(8,128)(2,1)S(1)} %collective-permute-done.9.refs_8_.refs_6_), channel_id=1, source_target_pairs={{1,0},{0,1},{17,16},{16,17},{33,32},{32,33},{49,48},{48,49},{5,4},... | collective-permute-start | bytes 1179656 | tf_op jit(solution)/shard_map/ppermute | solution.py:74
  23.8 7.8 %collective-permute-done.6.refs_2_ = bf16[384,512]{1,0:T(8,128)(2,1)S(1)} collective-permute-done((bf16[384,512]{1,0:T(8,128)(2,1)S(1)}, bf16[384,512]{1,0:T(8,128)(2,1)S(1)}, u32[]{:S(2)}, u32[]{:S(2)}) %collective-permute-start.6) | collective-permute-done | bytes 393248 | tf_op jit(solution)/shard_map/ppermute | solution.py:74
  31.6 1.8 %collective-permute-start.20 = (bf16[384,512]{1,0:T(8,128)(2,1)S(1)}, bf16[384,512]{1,0:T(8,128)(2,1)S(1)}, u32[]{:S(2)}, u32[]{:S(2)}) collective-permute-start(bf16[384,512]{1,0:T(8,128)(2,1)S(1)} %collective-permute-done.6.refs_2_), channel_id=1, source_target_pairs={{1,0},{0,1},{17,16},{16,17},{33,32},{32,33},{49,48},{48,49},{5,4},... | collective-permute-start | bytes 1179656 | tf_op jit(solution)/shard_map/ppermute | solution.py:74
  33.4 1.5 %collective-permute-start.4 = (bf16[384,512]{1,0:T(8,128)(2,1)S(1)}, bf16[384,512]{1,0:T(8,128)(2,1)S(1)}, u32[]{:S(2)}, u32[]{:S(2)}) collective-permute-start(bf16[384,512]{1,0:T(8,128)(2,1)S(1)} %collective-permute-done.3.refs_4_.refs_2_), channel_id=1, source_target_pairs={{48,0},{49,1},{0,16},{1,17},{16,32},{17,33},{32,48},{33,49},{52,4}... | collective-permute-start | bytes 1179656 | tf_op jit(solution)/shard_map/ppermute | solution.py:74
  35.1 1.3 %collective-permute-start.7 = (bf16[384,512]{1,0:T(8,128)(2,1)S(1)}, bf16[384,512]{1,0:T(8,128)(2,1)S(1)}, u32[]{:S(2)}, u32[]{:S(2)}) collective-permute-start(bf16[384,512]{1,0:T(8,128)(2,1)S(1)} %collective-permute-done.6.refs_2_), channel_id=1, source_target_pairs={{12,0},{13,1},{28,16},{29,17},{44,32},{45,33},{60,48},{61,49},{0,4... | collective-permute-start | bytes 1179656 | tf_op jit(solution)/shard_map/ppermute | solution.py:74
  36.4 7.7 %collective-permute-done.14.refs_10_.refs_8_ = bf16[384,512]{1,0:T(8,128)(2,1)S(1)} collective-permute-done((bf16[384,512]{1,0:T(8,128)(2,1)S(1)}, bf16[384,512]{1,0:T(8,128)(2,1)S(1)}, u32[]{:S(2)}, u32[]{:S(2)}) %collective-permute-start.14) | collective-permute-done | bytes 393248 | tf_op jit(solution)/shard_map/ppermute | solution.py:74
  44.1 1.1 %collective-permute-done.4.refs_12_.refs_10_.refs_2_ = bf16[384,512]{1,0:T(8,128)(2,1)S(1)} collective-permute-done((bf16[384,512]{1,0:T(8,128)(2,1)S(1)}, bf16[384,512]{1,0:T(8,128)(2,1)S(1)}, u32[]{:S(2)}, u32[]{:S(2)}) %collective-permute-start.4) | collective-permute-done | bytes 393248 | tf_op jit(solution)/shard_map/ppermute | solution.py:74
  45.2 1.0 %collective-permute-start.15 = (bf16[384,512]{1,0:T(8,128)(2,1)S(1)}, bf16[384,512]{1,0:T(8,128)(2,1)S(1)}, u32[]{:S(2)}, u32[]{:S(2)}) collective-permute-start(bf16[384,512]{1,0:T(8,128)(2,1)S(1)} %collective-permute-done.14.refs_10_.refs_8_), channel_id=1, source_target_pairs={{1,0},{0,1},{17,16},{16,17},{33,32},{32,33},{49,48},{48,49},{5,4},... | collective-permute-start | bytes 1179656 | tf_op jit(solution)/shard_map/ppermute | solution.py:74
  46.4 1.4 %collective-permute-start.17 = (bf16[384,512]{1,0:T(8,128)(2,1)S(1)}, bf16[384,512]{1,0:T(8,128)(2,1)S(1)}, u32[]{:S(2)}, u32[]{:S(2)}) collective-permute-start(bf16[384,512]{1,0:T(8,128)(2,1)S(1)} %collective-permute-done.16.refs_14_.refs_12_), channel_id=1, source_target_pairs={{1,0},{0,1},{17,16},{16,17},{33,32},{32,33},{49,48},{48,49},{5,4},... | collective-permute-start | bytes 1179656 | tf_op jit(solution)/shard_map/ppermute | solution.py:74
  47.9 7.2 %collective-permute-done.10.refs_6_ = bf16[384,512]{1,0:T(8,128)(2,1)S(1)} collective-permute-done((bf16[384,512]{1,0:T(8,128)(2,1)S(1)}, bf16[384,512]{1,0:T(8,128)(2,1)S(1)}, u32[]{:S(2)}, u32[]{:S(2)}) %collective-permute-start.10) | collective-permute-done | bytes 393248 | tf_op jit(solution)/shard_map/ppermute | solution.py:74
  55.1 1.7 %collective-permute-start.19 = (bf16[384,512]{1,0:T(8,128)(2,1)S(1)}, bf16[384,512]{1,0:T(8,128)(2,1)S(1)}, u32[]{:S(2)}, u32[]{:S(2)}) collective-permute-start(bf16[384,512]{1,0:T(8,128)(2,1)S(1)} %collective-permute-done.18.refs_14_), channel_id=1, source_target_pairs={{1,0},{0,1},{17,16},{16,17},{33,32},{32,33},{49,48},{48,49},{5,4},... | collective-permute-start | bytes 1179656 | tf_op jit(solution)/shard_map/ppermute | solution.py:74
  56.9 3.1 %shard_map.19.refs_12_ = f32[2,16,192]{2,1,0:T(8,128)S(1)} custom-call(bf16[384,512]{1,0:T(8,128)(2,1)S(1)} %get-tuple-element.17.refs_0_, bf16[384,512]{1,0:T(8,128)(2,1)S(1)} %get-tuple-element.18.refs_1_, bf16[384,512]{1,0:T(8,128)(2,1)S(1)} %collective-permute-done.6.refs_2_, bf16[384,512]{1,0:T(8,128)(2,1)S(1)} %collective-permute-done.20.refs_3_, ...), custom_call_target="tpu_custom_call" | custom-call | flops 1660944384 | bytes 1048576 | tf_op jit(solution)/shard_map/pallas_call | solution.py:257
  59.9 1.5 %shard_map.20.refs_16_ = f32[2,16,192]{2,1,0:T(8,128)S(1)} custom-call(bf16[384,512]{1,0:T(8,128)(2,1)S(1)} %get-tuple-element.17.refs_0_, bf16[384,512]{1,0:T(8,128)(2,1)S(1)} %get-tuple-element.18.refs_1_, bf16[384,512]{1,0:T(8,128)(2,1)S(1)} %collective-permute-done.6.refs_2_, bf16[384,512]{1,0:T(8,128)(2,1)S(1)} %collective-permute-done.20.refs_3_, ...), custom_call_target="tpu_custom_call" | custom-call | flops 754974720 | bytes 1048576 | tf_op jit(solution)/shard_map/pallas_call | solution.py:257
  61.4 2.2 %shard_map.21.refs_18_ = f32[2,16,192]{2,1,0:T(8,128)S(1)} custom-call(bf16[384,512]{1,0:T(8,128)(2,1)S(1)} %get-tuple-element.17.refs_0_, bf16[384,512]{1,0:T(8,128)(2,1)S(1)} %get-tuple-element.18.refs_1_, bf16[384,512]{1,0:T(8,128)(2,1)S(1)} %collective-permute-done.6.refs_2_, bf16[384,512]{1,0:T(8,128)(2,1)S(1)} %collective-permute-done.20.refs_3_, ...), custom_call_target="tpu_custom_call" | custom-call | flops 1056964608 | bytes 1048576 | tf_op jit(solution)/shard_map/pallas_call | solution.py:257
  63.6 2.6 %shard_map.22.refs_8_ = f32[2,16,192]{2,1,0:T(8,128)S(1)} custom-call(bf16[384,512]{1,0:T(8,128)(2,1)S(1)} %get-tuple-element.17.refs_0_, bf16[384,512]{1,0:T(8,128)(2,1)S(1)} %get-tuple-element.18.refs_1_, bf16[384,512]{1,0:T(8,128)(2,1)S(1)} %collective-permute-done.3.refs_4_.refs_2_, bf16[384,512]{1,0:T(8,128)(2,1)S(1)} %collective-permute-done.12.refs_5_.refs_3_, ...), custom_call_target="tpu_custom_call" | custom-call | flops 1509949440 | bytes 1048576 | tf_op jit(solution)/shard_map/pallas_call | solution.py:257
  66.3 1.3 %shard_map.23 = (f32[2,192]{1,0:T(2,128)S(1)}, f32[2,8,192]{2,1,0:T(8,128)S(1)}, f32[2,8,192]{2,1,0:T(8,128)S(1)}) custom-call(bf16[384,512]{1,0:T(8,128)(2,1)S(1)} %collective-permute-done.1.refs_6_.refs_4_.refs_0_, bf16[384,512]{1,0:T(8,128)(2,1)S(1)} %collective-permute-done.2.refs_7_.refs_5_.refs_1_, ...), custom_call_target="tpu_custom_call" | custom-call | flops 452984832 | bytes 1048576 | tf_op jit(solution)/shard_map/pallas_call | solution.py:257
  69.0 1.3 %collective-permute-start.23 = (f32[2,192]{1,0:T(2,128)S(1)}, f32[2,192]{1,0:T(2,128)S(1)}, u32[]{:S(2)}, u32[]{:S(2)}) collective-permute-start(f32[2,192]{1,0:T(2,128)S(1)} %get-tuple-element.23), channel_id=1, source_target_pairs={{0,126},{1,61},{16,78},{17,13},{32,94},{33,29},{48,110},{49,45},{4... | collective-permute-start | bytes 4616 | tf_op jit(solution)/shard_map/ppermute | solution.py:83
  70.4 1.9 %collective-permute-start.24 = (f32[2,192]{1,0:T(2,128)S(1)}, f32[2,192]{1,0:T(2,128)S(1)}, u32[]{:S(2)}, u32[]{:S(2)}) collective-permute-start(f32[2,192]{1,0:T(2,128)S(1)} %get-tuple-element.24), channel_id=1, source_target_pairs={{0,8},{1,83},{16,24},{17,99},{32,40},{33,115},{48,56},{49,67},{4,1... | collective-permute-start | bytes 4616 | tf_op jit(solution)/shard_map/ppermute | solution.py:83
  72.3 1.6 %collective-permute-start.25 = (f32[2,192]{1,0:T(2,128)S(1)}, f32[2,192]{1,0:T(2,128)S(1)}, u32[]{:S(2)}, u32[]{:S(2)}) collective-permute-start(f32[2,192]{1,0:T(2,128)S(1)} %get-tuple-element.25), channel_id=1, source_target_pairs={{0,18},{1,51},{16,34},{17,3},{32,50},{33,19},{48,2},{49,35},{4,22}... | collective-permute-start | bytes 4616 | tf_op jit(solution)/shard_map/ppermute | solution.py:83
  73.9 1.3 %collective-permute-start.26 = (f32[2,192]{1,0:T(2,128)S(1)}, f32[2,192]{1,0:T(2,128)S(1)}, u32[]{:S(2)}, u32[]{:S(2)}) collective-permute-start(f32[2,192]{1,0:T(2,128)S(1)} %get-tuple-element.26), channel_id=1, source_target_pairs={{0,2},{1,5},{16,18},{17,21},{32,34},{33,37},{48,50},{49,53},{4,6},... | collective-permute-start | bytes 4616 | tf_op jit(solution)/shard_map/ppermute | solution.py:83
  75.3 1.6 %collective-permute-done.25.refs_3_ = f32[2,192]{1,0:T(2,128)S(1)} collective-permute-done((f32[2,192]{1,0:T(2,128)S(1)}, f32[2,192]{1,0:T(2,128)S(1)}, u32[]{:S(2)}, u32[]{:S(2)}) %collective-permute-start.25) | collective-permute-done | bytes 1568 | tf_op jit(solution)/shard_map/ppermute | solution.py:83
  77.6 3.0 %collective-permute-start.27 = (f32[1,192]{1,0:T(1,128)S(1)}, f32[1,192]{1,0:T(1,128)S(1)}, u32[]{:S(2)}, u32[]{:S(2)}) collective-permute-start(f32[1,192]{1,0:T(1,128)S(1)} %get-tuple-element.28), channel_id=1, source_target_pairs={{1,0},{0,1},{17,16},{16,17},{33,32},{32,33},{49,48},{48,49},{5,4},... | collective-permute-start | bytes 2312 | tf_op jit(solution)/shard_map/ppermute | solution.py:74
  (36 shorter events, 5.1 us)
Async XLA Ops:
  0.0 2.9 %collective-permute-start = (bf16[384,512]{1,0:T(8,128)(2,1)}, bf16[384,512]{1,0:T(8,128)(2,1)S(1)}, u32[]{:S(2)}, u32[]{:S(2)}) collective-permute-start(bf16[384,512]{1,0:T(8,128)(2,1)} %in_ref.1), channel_id=1, source_target_pairs={{1,0},{0,1},{17,16},{16,17},{33,32},{32,33},{49,48},{48,49},{5,4},... | collective-permute-start | bytes 1179656 | tf_op jit(solution)/shard_map/ppermute | solution.py:74
  1.4 1.0 %copy-start = (bf16[384,512]{1,0:T(8,128)(2,1)S(1)}, bf16[384,512]{1,0:T(8,128)(2,1)}, u32[]{:S(2)}) copy-start(bf16[384,512]{1,0:T(8,128)(2,1)} %in_ref.1) | copy-start | bytes 1179652
  3.4 11.0 %collective-permute-start.1 = (bf16[384,512]{1,0:T(8,128)(2,1)S(1)}, bf16[384,512]{1,0:T(8,128)(2,1)S(1)}, u32[]{:S(2)}, u32[]{:S(2)}) collective-permute-start(bf16[384,512]{1,0:T(8,128)(2,1)S(1)} %get-tuple-element.17.refs_0_), channel_id=1, source_target_pairs={{4,0},{5,1},{20,16},{21,17},{36,32},{37,33},{52,48},{53,49},{8,4},... | collective-permute-start | bytes 1179656 | tf_op jit(solution)/shard_map/ppermute | solution.py:74
  6.3 10.3 %collective-permute-start.3 = (bf16[384,512]{1,0:T(8,128)(2,1)S(1)}, bf16[384,512]{1,0:T(8,128)(2,1)S(1)}, u32[]{:S(2)}, u32[]{:S(2)}) collective-permute-start(bf16[384,512]{1,0:T(8,128)(2,1)S(1)} %get-tuple-element.17.refs_0_), channel_id=1, source_target_pairs={{2,0},{3,1},{18,16},{19,17},{34,32},{35,33},{50,48},{51,49},{6,4},... | collective-permute-start | bytes 1179656 | tf_op jit(solution)/shard_map/ppermute | solution.py:74
  8.8 11.8 %collective-permute-start.9 = (bf16[384,512]{1,0:T(8,128)(2,1)S(1)}, bf16[384,512]{1,0:T(8,128)(2,1)S(1)}, u32[]{:S(2)}, u32[]{:S(2)}) collective-permute-start(bf16[384,512]{1,0:T(8,128)(2,1)S(1)} %get-tuple-element.17.refs_0_), channel_id=1, source_target_pairs={{82,0},{83,1},{98,16},{99,17},{114,32},{115,33},{66,48},{67,49},{8... | collective-permute-start | bytes 1179656 | tf_op jit(solution)/shard_map/ppermute | solution.py:74
  11.2 20.4 %collective-permute-start.6 = (bf16[384,512]{1,0:T(8,128)(2,1)S(1)}, bf16[384,512]{1,0:T(8,128)(2,1)S(1)}, u32[]{:S(2)}, u32[]{:S(2)}) collective-permute-start(bf16[384,512]{1,0:T(8,128)(2,1)S(1)} %get-tuple-element.17.refs_0_), channel_id=1, source_target_pairs={{126,0},{127,1},{78,16},{79,17},{94,32},{95,33},{110,48},{111,49},... | collective-permute-start | bytes 1179656 | tf_op jit(solution)/shard_map/ppermute | solution.py:74
  14.4 19.0 %collective-permute-start.2 = (bf16[384,512]{1,0:T(8,128)(2,1)S(1)}, bf16[384,512]{1,0:T(8,128)(2,1)S(1)}, u32[]{:S(2)}, u32[]{:S(2)}) collective-permute-start(bf16[384,512]{1,0:T(8,128)(2,1)S(1)} %collective-permute-done.1.refs_6_.refs_4_.refs_0_), channel_id=1, source_target_pairs={{1,0},{0,1},{17,16},{16,17},{33,32},{32,33},{49,48},{48,49},{5,4},... | collective-permute-start | bytes 1179656 | tf_op jit(solution)/shard_map/ppermute | solution.py:74
  16.6 18.3 %collective-permute-start.12 = (bf16[384,512]{1,0:T(8,128)(2,1)S(1)}, bf16[384,512]{1,0:T(8,128)(2,1)S(1)}, u32[]{:S(2)}, u32[]{:S(2)}) collective-permute-start(bf16[384,512]{1,0:T(8,128)(2,1)S(1)} %collective-permute-done.3.refs_4_.refs_2_), channel_id=1, source_target_pairs={{1,0},{0,1},{17,16},{16,17},{33,32},{32,33},{49,48},{48,49},{5,4},... | collective-permute-start | bytes 1179656 | tf_op jit(solution)/shard_map/ppermute | solution.py:74
  20.6 14.5 %collective-permute-start.13 = (bf16[384,512]{1,0:T(8,128)(2,1)S(1)}, bf16[384,512]{1,0:T(8,128)(2,1)S(1)}, u32[]{:S(2)}, u32[]{:S(2)}) collective-permute-start(bf16[384,512]{1,0:T(8,128)(2,1)S(1)} %collective-permute-done.9.refs_8_.refs_6_), channel_id=1, source_target_pairs={{1,0},{0,1},{17,16},{16,17},{33,32},{32,33},{49,48},{48,49},{5,4},... | collective-permute-start | bytes 1179656 | tf_op jit(solution)/shard_map/ppermute | solution.py:74
  31.6 4.7 %collective-permute-start.20 = (bf16[384,512]{1,0:T(8,128)(2,1)S(1)}, bf16[384,512]{1,0:T(8,128)(2,1)S(1)}, u32[]{:S(2)}, u32[]{:S(2)}) collective-permute-start(bf16[384,512]{1,0:T(8,128)(2,1)S(1)} %collective-permute-done.6.refs_2_), channel_id=1, source_target_pairs={{1,0},{0,1},{17,16},{16,17},{33,32},{32,33},{49,48},{48,49},{5,4},... | collective-permute-start | bytes 1179656 | tf_op jit(solution)/shard_map/ppermute | solution.py:74
  33.4 10.7 %collective-permute-start.14 = (bf16[384,512]{1,0:T(8,128)(2,1)S(1)}, bf16[384,512]{1,0:T(8,128)(2,1)S(1)}, u32[]{:S(2)}, u32[]{:S(2)}) collective-permute-start(bf16[384,512]{1,0:T(8,128)(2,1)S(1)} %collective-permute-done.3.refs_4_.refs_2_), channel_id=1, source_target_pairs={{16,0},{17,1},{32,16},{33,17},{48,32},{49,33},{0,48},{1,49},{20,4}... | collective-permute-start | bytes 1179656 | tf_op jit(solution)/shard_map/ppermute | solution.py:74
  33.4 11.8 %collective-permute-start.4 = (bf16[384,512]{1,0:T(8,128)(2,1)S(1)}, bf16[384,512]{1,0:T(8,128)(2,1)S(1)}, u32[]{:S(2)}, u32[]{:S(2)}) collective-permute-start(bf16[384,512]{1,0:T(8,128)(2,1)S(1)} %collective-permute-done.3.refs_4_.refs_2_), channel_id=1, source_target_pairs={{48,0},{49,1},{0,16},{1,17},{16,32},{17,33},{32,48},{33,49},{52,4}... | collective-permute-start | bytes 1179656 | tf_op jit(solution)/shard_map/ppermute | solution.py:74
  34.9 11.3 %collective-permute-start.16 = (bf16[384,512]{1,0:T(8,128)(2,1)S(1)}, bf16[384,512]{1,0:T(8,128)(2,1)S(1)}, u32[]{:S(2)}, u32[]{:S(2)}) collective-permute-start(bf16[384,512]{1,0:T(8,128)(2,1)S(1)} %collective-permute-done.1.refs_6_.refs_4_.refs_0_), channel_id=1, source_target_pairs={{4,0},{5,1},{20,16},{21,17},{36,32},{37,33},{52,48},{53,49},{8,4},... | collective-permute-start | bytes 1179656 | tf_op jit(solution)/shard_map/ppermute | solution.py:74
  35.1 11.4 %collective-permute-start.7 = (bf16[384,512]{1,0:T(8,128)(2,1)S(1)}, bf16[384,512]{1,0:T(8,128)(2,1)S(1)}, u32[]{:S(2)}, u32[]{:S(2)}) collective-permute-start(bf16[384,512]{1,0:T(8,128)(2,1)S(1)} %collective-permute-done.6.refs_2_), channel_id=1, source_target_pairs={{12,0},{13,1},{28,16},{29,17},{44,32},{45,33},{60,48},{61,49},{0,4... | collective-permute-start | bytes 1179656 | tf_op jit(solution)/shard_map/ppermute | solution.py:74
  36.4 11.4 %collective-permute-start.18 = (bf16[384,512]{1,0:T(8,128)(2,1)S(1)}, bf16[384,512]{1,0:T(8,128)(2,1)S(1)}, u32[]{:S(2)}, u32[]{:S(2)}) collective-permute-start(bf16[384,512]{1,0:T(8,128)(2,1)S(1)} %collective-permute-done.6.refs_2_), channel_id=1, source_target_pairs={{2,0},{3,1},{18,16},{19,17},{34,32},{35,33},{50,48},{51,49},{6,4},... | collective-permute-start | bytes 1179656 | tf_op jit(solution)/shard_map/ppermute | solution.py:74
  44.1 11.0 %collective-permute-start.10 = (bf16[384,512]{1,0:T(8,128)(2,1)S(1)}, bf16[384,512]{1,0:T(8,128)(2,1)S(1)}, u32[]{:S(2)}, u32[]{:S(2)}) collective-permute-start(bf16[384,512]{1,0:T(8,128)(2,1)S(1)} %collective-permute-done.9.refs_8_.refs_6_), channel_id=1, source_target_pairs={{66,0},{67,1},{82,16},{83,17},{98,32},{99,33},{114,48},{115,49},{7... | collective-permute-start | bytes 1179656 | tf_op jit(solution)/shard_map/ppermute | solution.py:74
  45.2 11.6 %collective-permute-start.15 = (bf16[384,512]{1,0:T(8,128)(2,1)S(1)}, bf16[384,512]{1,0:T(8,128)(2,1)S(1)}, u32[]{:S(2)}, u32[]{:S(2)}) collective-permute-start(bf16[384,512]{1,0:T(8,128)(2,1)S(1)} %collective-permute-done.14.refs_10_.refs_8_), channel_id=1, source_target_pairs={{1,0},{0,1},{17,16},{16,17},{33,32},{32,33},{49,48},{48,49},{5,4},... | collective-permute-start | bytes 1179656 | tf_op jit(solution)/shard_map/ppermute | solution.py:74
  46.2 15.2 %collective-permute-start.5 = (bf16[384,512]{1,0:T(8,128)(2,1)S(1)}, bf16[384,512]{1,0:T(8,128)(2,1)S(1)}, u32[]{:S(2)}, u32[]{:S(2)}) collective-permute-start(bf16[384,512]{1,0:T(8,128)(2,1)S(1)} %collective-permute-done.4.refs_12_.refs_10_.refs_2_), channel_id=1, source_target_pairs={{1,0},{0,1},{17,16},{16,17},{33,32},{32,33},{49,48},{48,49},{5,4},... | collective-permute-start | bytes 1179656 | tf_op jit(solution)/shard_map/ppermute | solution.py:74
  46.4 15.0 %collective-permute-start.17 = (bf16[384,512]{1,0:T(8,128)(2,1)S(1)}, bf16[384,512]{1,0:T(8,128)(2,1)S(1)}, u32[]{:S(2)}, u32[]{:S(2)}) collective-permute-start(bf16[384,512]{1,0:T(8,128)(2,1)S(1)} %collective-permute-done.16.refs_14_.refs_12_), channel_id=1, source_target_pairs={{1,0},{0,1},{17,16},{16,17},{33,32},{32,33},{49,48},{48,49},{5,4},... | collective-permute-start | bytes 1179656 | tf_op jit(solution)/shard_map/ppermute | solution.py:74
  47.8 15.8 %collective-permute-start.8 = (bf16[384,512]{1,0:T(8,128)(2,1)S(1)}, bf16[384,512]{1,0:T(8,128)(2,1)S(1)}, u32[]{:S(2)}, u32[]{:S(2)}) collective-permute-start(bf16[384,512]{1,0:T(8,128)(2,1)S(1)} %collective-permute-done.7.refs_16_.refs_4_), channel_id=1, source_target_pairs={{1,0},{0,1},{17,16},{16,17},{33,32},{32,33},{49,48},{48,49},{5,4},... | collective-permute-start | bytes 1179656 | tf_op jit(solution)/shard_map/ppermute | solution.py:74
  55.1 8.5 %collective-permute-start.19 = (bf16[384,512]{1,0:T(8,128)(2,1)S(1)}, bf16[384,512]{1,0:T(8,128)(2,1)S(1)}, u32[]{:S(2)}, u32[]{:S(2)}) collective-permute-start(bf16[384,512]{1,0:T(8,128)(2,1)S(1)} %collective-permute-done.18.refs_14_), channel_id=1, source_target_pairs={{1,0},{0,1},{17,16},{16,17},{33,32},{32,33},{49,48},{48,49},{5,4},... | collective-permute-start | bytes 1179656 | tf_op jit(solution)/shard_map/ppermute | solution.py:74
  56.9 9.4 %collective-permute-start.11 = (bf16[384,512]{1,0:T(8,128)(2,1)S(1)}, bf16[384,512]{1,0:T(8,128)(2,1)S(1)}, u32[]{:S(2)}, u32[]{:S(2)}) collective-permute-start(bf16[384,512]{1,0:T(8,128)(2,1)S(1)} %collective-permute-done.10.refs_6_), channel_id=1, source_target_pairs={{1,0},{0,1},{17,16},{16,17},{33,32},{32,33},{49,48},{48,49},{5,4},... | collective-permute-start | bytes 1179656 | tf_op jit(solution)/shard_map/ppermute | solution.py:74
  67.6 1.4 %collective-permute-start.21 = (f32[2,8,192]{2,1,0:T(8,128)S(1)}, f32[2,8,192]{2,1,0:T(8,128)S(1)}, u32[]{:S(2)}, u32[]{:S(2)}) collective-permute-start(f32[2,8,192]{2,1,0:T(8,128)S(1)} %get-tuple-element.21), channel_id=1, source_target_pairs={{1,0},{0,1},{17,16},{16,17},{33,32},{32,33},{49,48},{48,49},{5,4},... | collective-permute-start | bytes 36872 | tf_op jit(solution)/shard_map/ppermute | solution.py:74
  68.9 6.3 %collective-permute-start.22 = (f32[2,192]{1,0:T(2,128)S(1)}, f32[2,192]{1,0:T(2,128)S(1)}, u32[]{:S(2)}, u32[]{:S(2)}) collective-permute-start(f32[2,192]{1,0:T(2,128)S(1)} %get-tuple-element.22), channel_id=1, source_target_pairs={{0,122},{1,81},{16,74},{17,97},{32,90},{33,113},{48,106},{49,65},{... | collective-permute-start | bytes 4616 | tf_op jit(solution)/shard_map/ppermute | solution.py:83
  69.0 6.2 %collective-permute-start.23 = (f32[2,192]{1,0:T(2,128)S(1)}, f32[2,192]{1,0:T(2,128)S(1)}, u32[]{:S(2)}, u32[]{:S(2)}) collective-permute-start(f32[2,192]{1,0:T(2,128)S(1)} %get-tuple-element.23), channel_id=1, source_target_pairs={{0,126},{1,61},{16,78},{17,13},{32,94},{33,29},{48,110},{49,45},{4... | collective-permute-start | bytes 4616 | tf_op jit(solution)/shard_map/ppermute | solution.py:83
  70.4 4.9 %collective-permute-start.24 = (f32[2,192]{1,0:T(2,128)S(1)}, f32[2,192]{1,0:T(2,128)S(1)}, u32[]{:S(2)}, u32[]{:S(2)}) collective-permute-start(f32[2,192]{1,0:T(2,128)S(1)} %get-tuple-element.24), channel_id=1, source_target_pairs={{0,8},{1,83},{16,24},{17,99},{32,40},{33,115},{48,56},{49,67},{4,1... | collective-permute-start | bytes 4616 | tf_op jit(solution)/shard_map/ppermute | solution.py:83
  72.3 4.5 %collective-permute-start.25 = (f32[2,192]{1,0:T(2,128)S(1)}, f32[2,192]{1,0:T(2,128)S(1)}, u32[]{:S(2)}, u32[]{:S(2)}) collective-permute-start(f32[2,192]{1,0:T(2,128)S(1)} %get-tuple-element.25), channel_id=1, source_target_pairs={{0,18},{1,51},{16,34},{17,3},{32,50},{33,19},{48,2},{49,35},{4,22}... | collective-permute-start | bytes 4616 | tf_op jit(solution)/shard_map/ppermute | solution.py:83
  73.9 3.6 %collective-permute-start.26 = (f32[2,192]{1,0:T(2,128)S(1)}, f32[2,192]{1,0:T(2,128)S(1)}, u32[]{:S(2)}, u32[]{:S(2)}) collective-permute-start(f32[2,192]{1,0:T(2,128)S(1)} %get-tuple-element.26), channel_id=1, source_target_pairs={{0,2},{1,5},{16,18},{17,21},{32,34},{33,37},{48,50},{49,53},{4,6},... | collective-permute-start | bytes 4616 | tf_op jit(solution)/shard_map/ppermute | solution.py:83
  77.6 3.9 %collective-permute-start.27 = (f32[1,192]{1,0:T(1,128)S(1)}, f32[1,192]{1,0:T(1,128)S(1)}, u32[]{:S(2)}, u32[]{:S(2)}) collective-permute-start(f32[1,192]{1,0:T(1,128)S(1)} %get-tuple-element.28), channel_id=1, source_target_pairs={{1,0},{0,1},{17,16},{16,17},{33,32},{32,33},{49,48},{48,49},{5,4},... | collective-permute-start | bytes 2312 | tf_op jit(solution)/shard_map/ppermute | solution.py:74
